TPU v7x, 32 devices: a whole 2x2x4 slice. The times are simulated.
32 devices in a mesh: grp: 4 (over y, x), row: 8 (over z, core).
Axes of the slice: x: 2, y: 2, z: 4, core: 2. Of those that a mesh axis runs over, the one named last changes fastest.
Arguments:
- krylov_basis: bfloat16 [300, 512, 512], P(None, 'row', 'grp'), may hold values from -30 to 30
- krylov_image: bfloat16 [300, 512, 512], P(None, 'row', 'grp'), may hold values from -30 to 30
- tridiag_vectors: bfloat16 [300, 32], P(None, 'grp'), may hold values from -0.375 to 0.375
- ritz_values: bfloat16 [32], P('grp'), may hold values from -3 to 3
Outputs:
- ritz_vectors: float32 [32, 512, 512], P('grp', 'row')
- ritz_residuals: float32 [32, 512, 512], P('grp', 'row')
- residual_norms: float32 [32], P('grp')
All inputs are finite; a program needn't handle non-finite values.
Results may differ from a plain program's by a relative error of at most 0.0003.
Values may be sent and summed in bfloat16 or wider, within the bound.
A program may use at most 64 MiB of HBM per device.

v0:
```python
import functools
import math

import jax
import jax.numpy as jnp
from jax import lax
from jax.experimental import pallas as pl
from jax.experimental.pallas import tpu as pltpu
from jax.sharding import PartitionSpec as P

MESH = pl.DeviceIdType.MESH
MIB = 1 << 20
TILE = 8
STEP = 16
LANES = 128
SPREAD = 256.0
REACH = 86.0
SLOPE = 2.0 * REACH / math.log(1.0 + SPREAD)
LEAST = 1e-35


def cdiv(a, b):
    return (a + b - 1) // b


def grid_iota(shape, dim):
    return lax.broadcasted_iota(jnp.int32, shape, dim)


def expand_rows(cols, width):
    return jnp.broadcast_to(cols, (cols.shape[0], width)).reshape(cols.shape[0], 1, width)


def exchange_kernel(
    groups, rows, krylov_len,
    tridiag_ref, values_ref, basis_ref, image_ref,
    coded_ref, stats_ref, total_ref,
    packed_ref, coefs, fields, spread, reps, expanded, coded, stat_send, stat_recv, square_send, square_recv,
    load_sem, coef_sems, data_sems, own_sem, stat_sems, square_sems,
):
    wanted_dev, packed_width = packed_ref.shape
    wanted = groups * wanted_dev
    chunks = fields.shape[1]
    inner_dev = basis_ref.shape[2]
    padded_len = fields.shape[2]
    steps = padded_len // STEP
    wide = STEP * TILE
    block = wanted_dev * TILE
    grp = lax.axis_index("grp")
    row = lax.axis_index("row")
    lane_stats = grid_iota((wanted, LANES), 1)

    def loads(chunk):
        span = pl.ds(pl.multiple_of(chunk * TILE, TILE), TILE)
        return [
            pltpu.make_async_copy(
                ref.at[:, span, :], fields.at[which, chunk, pl.ds(0, krylov_len)], load_sem.at[which, chunk]
            )
            for which, ref in enumerate((basis_ref, image_ref))
        ]

    for chunk in range(chunks):
        for copy in loads(chunk):
            copy.start()

    near = grid_iota((wanted_dev, wanted_dev), 0) == grid_iota((wanted_dev, wanted_dev), 1)
    own_values = jnp.broadcast_to(values_ref[...].astype(jnp.float32), (wanted_dev, wanted_dev))
    own_values = jnp.sum(jnp.where(near, own_values, 0.0), axis=1, keepdims=True)
    packed_ref[...] = jnp.broadcast_to(own_values, (wanted_dev, packed_width))
    packed_ref[:, :krylov_len] = tridiag_ref[...].astype(jnp.float32)

    barrier = pltpu.get_barrier_semaphore()
    def others(action):
        for across in range(groups):
            lax.fori_loop(1 if across == 0 else 0, rows, functools.partial(action, across), 0)

    def device(across, along):
        return {"grp": lax.rem(grp + across, groups), "row": lax.rem(row + along, rows)}

    def greet(across, along, carry):
        pl.semaphore_signal(barrier, inc=1, device_id=device(across, along), device_id_type=MESH)
        return carry

    others(greet)
    pl.semaphore_wait(barrier, groups * rows - 1)

    def remote(src, dst, sems, index, across, along=0):
        return pltpu.make_async_remote_copy(
            src_ref=src,
            dst_ref=dst,
            send_sem=sems.at[(0,) + index],
            recv_sem=sems.at[(1,) + index],
            device_id=device(across, along),
            device_id_type=MESH,
        )

    def coef_copy(step):
        return remote(packed_ref, coefs.at[grp], coef_sems, (step,), step)

    for step in range(1, groups):
        coef_copy(step).start()
    coefs[grp] = packed_ref[...]

    if padded_len > krylov_len:
        for chunk in range(chunks):
            for which in range(2):
                fields[which, chunk, pl.ds(krylov_len, padded_len - krylov_len)] = jnp.zeros(
                    (padded_len - krylov_len, TILE, inner_dev), jnp.bfloat16
                )
    shape = spread.shape
    spread[...] = jnp.where(
        lax.shift_right_logical(grid_iota(shape, 1), 3) == grid_iota(shape, 0), 1.0, 0.0
    ).astype(jnp.bfloat16)

    for step in range(1, groups):
        coef_copy(step).wait()

    all_coefs = coefs[...].reshape(wanted, packed_width)
    shift_values = expand_rows(all_coefs[:, packed_width - 1 :], inner_dev)
    for part in range(cdiv(padded_len, LANES)):
        reps[part] = jnp.dot(
            all_coefs[:, part * LANES : (part + 1) * LANES].astype(jnp.bfloat16),
            spread[...],
            preferred_element_type=jnp.float32,
        )
    per_part = LANES // STEP
    same = (grid_iota((TILE, wide), 1) & (TILE - 1)) == grid_iota((TILE, wide), 0)
    for step in range(steps):
        at = (step % per_part) * wide
        values = reps[step // per_part, :, at : at + wide]
        values = jnp.where(same[None], values.reshape(wanted, 1, wide), 0.0)
        expanded[:, step * wide : (step + 1) * wide] = values.reshape(wanted * TILE, wide).astype(jnp.bfloat16)

    def data_copy(chunk, step):
        dest = lax.rem(grp + step, groups)
        return remote(
            coded.at[chunk, pl.ds(pl.multiple_of(dest * block, block), block)],
            coded_ref.at[grp, chunk],
            data_sems, (chunk, step), step,
        )

    def own_copy(chunk):
        return pltpu.make_async_copy(
            coded.at[chunk, pl.ds(pl.multiple_of(grp * block, block), block)],
            coded_ref.at[grp, chunk],
            own_sem.at[chunk],
        )

    def stat_copy(step):
        return remote(
            stat_send.at[lax.rem(grp + step, groups)], stat_recv.at[grp], stat_sems, (step,), step
        )

    def square_copy(across, along):
        return remote(
            square_send.at[lax.rem(grp + across, groups)], square_recv.at[grp * rows + row],
            square_sems, (across, along), across, along,
        )

    def square_start(across, along, carry):
        square_copy(across, along).start()
        return carry

    def square_wait(across, along, carry):
        square_copy(across, along).wait()
        return carry

    column = grid_iota((wanted, LANES), 0) % wanted_dev

    def compute(chunk, carry):
        stats, sums = carry
        for copy in loads(chunk):
            copy.wait()
        both = jnp.concatenate(
            [fields[which, chunk].reshape(padded_len * TILE, inner_dev) for which in range(2)], axis=1
        )
        product = jnp.dot(expanded[...], both, preferred_element_type=jnp.float32)
        product = product.reshape(wanted, TILE, 2 * inner_dev)
        ritz = product[:, :, :inner_dev]
        resid = product[:, :, inner_dev:] - shift_values * ritz
        for kind, cols in enumerate((ritz, resid)):
            squares = jnp.sum(jnp.sum(cols * cols, axis=1), axis=1, keepdims=True)
            most = jnp.max(jnp.max(jnp.abs(cols), axis=1), axis=1, keepdims=True)
            most = jnp.maximum(most, LEAST)
            codes = jnp.exp(SLOPE * jnp.log(1.0 + jnp.abs(cols) * expand_rows(SPREAD / most, inner_dev)) - REACH)
            codes = jnp.where(cols < 0.0, -codes, codes)
            coded[chunk, :, kind * inner_dev : (kind + 1) * inner_dev] = codes.reshape(
                wanted * TILE, inner_dev
            ).astype(jnp.bfloat16)
            stats = jnp.where(lane_stats == 2 * chunk + kind, most, stats)
            sums = jnp.where(lane_stats == column + kind * wanted_dev, sums + squares, sums)

        @pl.when(chunk == chunks - 1)
        def _():
            square_send[...] = jnp.sum(sums.reshape(groups, wanted_dev, LANES), axis=1, keepdims=True)
            others(square_start)
            stat_send[...] = stats.reshape(groups, wanted_dev, LANES)
            for step in range(1, groups):
                stat_copy(step).start()

        for step in range(1, groups):
            data_copy(chunk, step).start()
        own_copy(chunk).start()
        return stats, sums

    nothing = jnp.zeros((wanted, LANES), jnp.float32)
    lax.fori_loop(0, chunks, compute, (nothing, nothing))

    for step in range(1, groups):
        stat_copy(step).wait()
    stat_recv[grp] = stat_send[grp]
    stats_ref[...] = stat_recv[...]
    others(square_wait)
    square_recv[grp * rows + row] = square_send[grp]
    total_ref[...] = jnp.sum(square_recv[...], axis=0)

    def finish(chunk, carry):
        for step in range(1, groups):
            data_copy(chunk, step).wait()
        own_copy(chunk).wait()
        return carry

    lax.fori_loop(0, chunks, finish, 0)


def finish_kernel(rows_total, coded_ref, stats_ref, total_ref, ritz_ref, resid_ref, norm_ref):
    groups, wanted_dev = stats_ref.shape[:2]
    several = coded_ref.shape[1]
    first = pl.program_id(0) * several
    inner_dev = coded_ref.shape[3] // 2
    lanes = grid_iota((wanted_dev, LANES), 1)
    columns = grid_iota((wanted_dev, LANES), 0)

    def pick(tile, lane):
        return jnp.sum(jnp.where(lanes == lane, tile, 0.0), axis=1, keepdims=True)

    total = jnp.broadcast_to(total_ref[...], (wanted_dev, LANES))
    ritz_squares = pick(total, columns) + 1.0
    resid_squares = pick(total, columns + wanted_dev)
    factor = jnp.sqrt(rows_total / ritz_squares)
    for source in range(groups):
        for part in range(several):
            for kind, out_ref in enumerate((ritz_ref, resid_ref)):
                scale = pick(stats_ref[source], 2 * (first + part) + kind) * (factor * (1.0 / SPREAD))
                codes = coded_ref[source, part, :, kind * inner_dev : (kind + 1) * inner_dev].astype(jnp.float32)
                size = jnp.exp((jnp.log(jnp.abs(codes)) + REACH) * (1.0 / SLOPE)) - 1.0
                size = jnp.where(codes < 0.0, -size, size)
                size = size.reshape(wanted_dev, TILE, inner_dev) * expand_rows(scale, inner_dev)
                out_ref[:, part * TILE : (part + 1) * TILE, source * inner_dev : (source + 1) * inner_dev] = size
    norms = jnp.broadcast_to(jnp.sqrt(resid_squares / ritz_squares), (wanted_dev, LANES))
    norm_ref[...] = jnp.sum(jnp.where(lanes == columns, norms, 0.0), axis=0)[:wanted_dev]


def body(groups, rows, krylov_basis, krylov_image, tridiag_vectors, ritz_values):
    krylov_len, outer_dev, inner_dev = krylov_basis.shape
    wanted_dev = tridiag_vectors.shape[1]
    wanted = groups * wanted_dev
    chunks = outer_dev // TILE
    block = wanted_dev * TILE
    padded_len = cdiv(krylov_len, STEP) * STEP
    packed_width = cdiv(padded_len + 1, LANES) * LANES
    rows_total = float(outer_dev * inner_dev * groups * rows)
    f32, bf16 = jnp.float32, jnp.bfloat16
    dma = pltpu.SemaphoreType.DMA
    anywhere = pl.BlockSpec(memory_space=pl.ANY)
    vmem = pl.BlockSpec(memory_space=pltpu.VMEM)
    hbm = pl.BlockSpec(memory_space=pltpu.HBM)
    parts = cdiv(padded_len, LANES)
    several = math.gcd(chunks, 4)
    coded, stats, total = pl.pallas_call(
        functools.partial(exchange_kernel, groups, rows, krylov_len),
        name="exchange",
        out_shape=(
            jax.ShapeDtypeStruct((groups, chunks, block, 2 * inner_dev), bf16),
            jax.ShapeDtypeStruct((groups, wanted_dev, LANES), f32),
            jax.ShapeDtypeStruct((1, LANES), f32),
        ),
        in_specs=[vmem, vmem, hbm, hbm],
        out_specs=(anywhere, vmem, vmem),
        scratch_shapes=[
            pltpu.VMEM((wanted_dev, packed_width), f32),
            pltpu.VMEM((groups, wanted_dev, packed_width), f32),
            pltpu.VMEM((2, chunks, padded_len, TILE, inner_dev), bf16),
            pltpu.VMEM((LANES, LANES * TILE), bf16),
            pltpu.VMEM((parts, wanted, LANES * TILE), f32),
            pltpu.VMEM((wanted * TILE, padded_len * TILE), bf16),
            pltpu.VMEM((chunks, wanted * TILE, 2 * inner_dev), bf16),
            pltpu.VMEM((groups, wanted_dev, LANES), f32),
            pltpu.VMEM((groups, wanted_dev, LANES), f32),
            pltpu.VMEM((groups, 1, LANES), f32),
            pltpu.VMEM((groups * rows, 1, LANES), f32),
            dma((2, chunks)),
            dma((2, groups)),
            dma((2, chunks, groups)),
            dma((chunks,)),
            dma((2, groups)),
            dma((2, groups, rows)),
        ],
        compiler_params=pltpu.CompilerParams(
            collective_id=0, has_side_effects=True, vmem_limit_bytes=52 * MIB
        ),
    )(tridiag_vectors.T, ritz_values[None], krylov_basis, krylov_image)
    ritz_vectors, ritz_residuals, norms = pl.pallas_call(
        functools.partial(finish_kernel, rows_total),
        name="finish",
        grid=(chunks // several,),
        out_shape=(
            jax.ShapeDtypeStruct((wanted_dev, outer_dev, groups * inner_dev), f32),
            jax.ShapeDtypeStruct((wanted_dev, outer_dev, groups * inner_dev), f32),
            jax.ShapeDtypeStruct((wanted_dev,), f32),
        ),
        in_specs=[
            pl.BlockSpec((groups, several, block, 2 * inner_dev), lambda c: (0, c, 0, 0)),
            pl.BlockSpec((groups, wanted_dev, LANES), lambda c: (0, 0, 0)),
            pl.BlockSpec((1, LANES), lambda c: (0, 0)),
        ],
        out_specs=(
            pl.BlockSpec((wanted_dev, several * TILE, groups * inner_dev), lambda c: (0, c, 0)),
            pl.BlockSpec((wanted_dev, several * TILE, groups * inner_dev), lambda c: (0, c, 0)),
            pl.BlockSpec((wanted_dev,), lambda c: (0,)),
        ),
        compiler_params=pltpu.CompilerParams(vmem_limit_bytes=16 * MIB),
    )(coded, stats, total)
    return ritz_vectors, ritz_residuals, norms


def solution(mesh):
    placed = (P(None, "row", "grp"), P(None, "row", "grp"), P(None, "grp"), P("grp"))
    return jax.shard_map(
        functools.partial(body, mesh.shape["grp"], mesh.shape["row"]),
        mesh=mesh,
        in_specs=placed,
        out_specs=(P("grp", "row", None), P("grp", "row", None), P("grp")),
        check_vma=False,
    )
```

profile of v0, /device:TPU:0, one launch (start us, length us, event | category | flops | bytes accessed | tf_op | source)
XLA Modules:
  0.0 30.3 jit_solution(8460399461764404166)
XLA Ops:
  0.6 0.0 copy-start
  0.6 0.7 %copy-done = bf16[300,8]{0,1:T(8,128)(2,1)S(1)} copy-done((bf16[300,8]{0,1:T(8,128)(2,1)S(1)}, bf16[300,8]{0,1:T(8,128)(2,1)}, u32[]{:S(2)}) %copy-start) | copy-done | bytes 4824
  1.3 0.0 copy-start.1
  1.3 0.7 %copy-done.1 = bf16[8]{0:T(256)(128)(2,1)S(1)} copy-done((bf16[8]{0:T(256)(128)(2,1)S(1)}, bf16[8]{0:T(256)(128)(2,1)}, u32[]{:S(2)}) %copy-start.1) | copy-done | bytes 40
  2.0 26.1 %exchange.1 = (bf16[4,8,64,256]{3,2,1,0:T(8,128)(2,1)S(1)}, f32[4,8,128]{2,1,0:T(8,128)S(1)}, f32[1,128]{1,0:T(1,128)S(1)}) custom-call(bf16[8,300]{1,0:T(8,128)(2,1)S(1)} %bitcast.2, bf16[1,8]{1,0:T(2,128)(2,1)S(1)} %bitcast.3, bf16[300,64,128]{2,1,0:T(8,128)(2,1)} %basis_ref.1, bf16[300,64,128]{2,1,0:T(8,128)(2,1)} %image_ref.1), custom_call_target="tpu_custom_call" | custom-call | tf_op jit(solution)/shard_map/exchange/pallas_call | solution.py:270
  28.1 2.1 %finish.1 = (f32[8,64,512]{2,1,0:T(8,128)}, f32[8,64,512]{2,1,0:T(8,128)}, f32[8]{0:T(128)}) custom-call(bf16[4,8,64,256]{3,2,1,0:T(8,128)(2,1)S(1)} %get-tuple-element.6.coded_ref, f32[4,8,128]{2,1,0:T(8,128)S(1)} %get-tuple-element.7.stats_ref, f32[1,128]{1,0:T(1,128)S(1)} %get-tuple-element.8.total_ref), custom_call_target="tpu_custom_call" | custom-call | tf_op jit(solution)/shard_map/finish/pallas_call | solution.py:303
Async XLA Ops:
  0.6 0.7 %copy-start = (bf16[300,8]{0,1:T(8,128)(2,1)S(1)}, bf16[300,8]{0,1:T(8,128)(2,1)}, u32[]{:S(2)}) copy-start(bf16[300,8]{0,1:T(8,128)(2,1)} %param.6) | copy-start | bytes 14404
  1.3 0.7 %copy-start.1 = (bf16[8]{0:T(256)(128)(2,1)S(1)}, bf16[8]{0:T(256)(128)(2,1)}, u32[]{:S(2)}) copy-start(bf16[8]{0:T(256)(128)(2,1)} %param.7) | copy-start | bytes 52
where the time goes:
time: 30.5 us; the launch traced here: 30.3 us
  Pallas kernels  28.3 us (93%)
  local copies, waits for them, and re-layouts  1.34 us (4%)
  between operations  0.65 us (2%)
    pallas_call x1, Pallas kernels, body(): pl.pallas_call(functools.partial(exchange_kernel, groups, rows, krylov_le...  26.1 us
    pallas_call x1, Pallas kernels, body(): pl.pallas_call(functools.partial(finish_kernel, rows_total), name='finish...  2.14 us
    unnamed x4, local copies, waits for them, and re-layouts  1.34 us

commit v1 on v0

v1 whole, which is shorter than its diff:
```python
import functools
import math

import jax
import jax.numpy as jnp
from jax import lax
from jax.experimental import pallas as pl
from jax.experimental.pallas import tpu as pltpu
from jax.sharding import PartitionSpec as P

MESH = pl.DeviceIdType.MESH
MIB = 1 << 20
TILE = 8
STEP = 16
LANES = 128
POWER = 13
PEAK = 2.0 ** (126.0 / POWER)
SHIFT = 2.0**30
LEAST = 1e-36


def cdiv(a, b):
    return (a + b - 1) // b


def grid_iota(shape, dim):
    return lax.broadcasted_iota(jnp.int32, shape, dim)


def expand_rows(cols, width):
    return jnp.broadcast_to(cols, (cols.shape[0], width)).reshape(cols.shape[0], 1, width)


def encode(cols, inverse):
    y = cols * inverse
    y2 = y * y
    y4 = y2 * y2
    y8 = y4 * y4
    return (y8 * y4) * y


def decode(codes):
    size = jnp.exp2(jnp.log(jnp.abs(codes)) * (1.0 / (POWER * math.log(2.0))))
    return jnp.where(codes < 0.0, -size, size)


def exchange_kernel(
    groups, rows,
    tridiag_ref, values_ref, basis_ref, image_ref,
    ritz_ref, resid_ref, total_ref,
    coefs, values, fields, spread, reps, expanded, coded, received,
    stat_send, stat_recv, square_send, square_recv,
    coef_load, coef_send, coef_recv, load_sem, data_sems, stat_sems, square_sems,
    ready_sem, plane_sem, go_sem,
):
    wanted_dev, krylov_len = tridiag_ref.shape
    chunks = fields.shape[1]
    padded_len = fields.shape[2]
    inner_dev = basis_ref.shape[2]
    steps = padded_len // STEP
    wide = STEP * TILE
    block = wanted_dev * TILE
    planes = rows // 2
    grp = lax.axis_index("grp")
    row = lax.axis_index("row")
    core = lax.rem(row, 2)
    plane = lax.div(row, 2)
    lead = core == 1

    def partner(mask):
        if mask == 0:
            return grp
        if mask == 1:
            return grp + 1 - 2 * lax.rem(grp, 2)
        if mask == 2:
            return lax.rem(grp + 2, groups)
        return groups - 1 - grp

    def device(mask, at_plane, at_core):
        return {"grp": partner(mask), "row": 2 * at_plane + at_core}

    def signal(sem, where):
        pl.semaphore_signal(sem, inc=1, device_id=where, device_id_type=MESH)

    barrier = pltpu.get_barrier_semaphore()
    for mask in (1, 2):
        signal(barrier, device(mask, plane, 1))

    coef_loads = [
        pltpu.make_async_copy(tridiag_ref, coefs.at[0], coef_load.at[0]),
        pltpu.make_async_copy(values_ref, values.at[0], coef_load.at[1]),
    ]
    for copy in coef_loads:
        copy.start()

    @pl.when(core == 0)
    def _():
        signal(barrier, device(0, plane, 1))

        def greet(ahead, carry):
            signal(barrier, device(0, lax.rem(plane + ahead, planes), 0))
            return carry

        lax.fori_loop(1, planes, greet, 0)

    def loads(chunk):
        span = pl.ds(pl.multiple_of(chunk * TILE, TILE), TILE)
        return [
            pltpu.make_async_copy(
                ref.at[:, span, :], fields.at[which, chunk, pl.ds(0, krylov_len)], load_sem.at[which, chunk]
            )
            for which, ref in enumerate((basis_ref, image_ref))
        ]

    for chunk in range(chunks):
        for copy in loads(chunk):
            copy.start()

    if padded_len > krylov_len:
        for chunk in range(chunks):
            for which in range(2):
                fields[which, chunk, pl.ds(krylov_len, padded_len - krylov_len)] = jnp.zeros(
                    (padded_len - krylov_len, TILE, inner_dev), jnp.bfloat16
                )
    shape = spread.shape
    spread[...] = jnp.where(
        lax.shift_right_logical(grid_iota(shape, 1), 3) == grid_iota(shape, 0), SHIFT, 0.0
    ).astype(jnp.bfloat16)

    for copy in coef_loads:
        copy.wait()

    def coef_copies(source, slot, number, mask, at_core):
        return [
            pltpu.make_async_remote_copy(
                src_ref=ref.at[source],
                dst_ref=ref.at[slot],
                send_sem=coef_send.at[number, kind],
                recv_sem=coef_recv.at[slot - 1, kind],
                device_id=device(mask, plane, at_core),
                device_id_type=MESH,
            )
            for kind, ref in enumerate((coefs, values))
        ]

    own_sends = [
        copy
        for mask in (1, 2)
        for at_core in (1, 0)
        for copy in coef_copies(0, mask, 2 * mask + at_core - 2, mask, at_core)
    ]
    relay_sends = [copy for at_core in (1, 0) for copy in coef_copies(1, 3, 4 + at_core, 2, at_core)]

    def coef_wait(slot):
        for copy in coef_copies(0, slot, 0, 1, 1):
            copy.wait_recv()

    @pl.when(lead)
    def _():
        pl.semaphore_wait(barrier, 5)
        for copy in own_sends:
            copy.start()
        signal(ready_sem, device(0, plane, 0))
        coef_wait(1)
        for copy in relay_sends:
            copy.start()
        coef_wait(2)

    @pl.when(core == 0)
    def _():
        pl.semaphore_wait(ready_sem, 1)
        coef_wait(1)
        coef_wait(2)

    near = grid_iota((wanted_dev, wanted_dev), 0) == grid_iota((wanted_dev, wanted_dev), 1)
    same = (grid_iota((TILE, wide), 1) & (TILE - 1)) == grid_iota((TILE, wide), 0)
    per_part = LANES // STEP
    pair = 2 * wanted_dev
    lane = grid_iota((pair, LANES), 1)

    def prepare(slots):
        shifts = []
        for slot in slots:
            spot = jnp.broadcast_to(values[slot].astype(jnp.float32), (wanted_dev, wanted_dev))
            shifts.append(jnp.sum(jnp.where(near, spot, 0.0), axis=1, keepdims=True))
        shift_values = expand_rows(jnp.concatenate(shifts, axis=0), inner_dev)
        both = jnp.concatenate([coefs[slot] for slot in slots], axis=0)
        for part in range(cdiv(krylov_len, LANES)):
            piece = both[:, part * LANES : min((part + 1) * LANES, krylov_len)]
            reps[part] = jnp.dot(piece, spread[: piece.shape[1]], preferred_element_type=jnp.float32)
        for step in range(steps):
            at = (step % per_part) * wide
            spot = reps[step // per_part, :, at : at + wide]
            spot = jnp.where(same[None], spot.reshape(pair, 1, wide), 0.0)
            expanded[:, step * wide : (step + 1) * wide] = spot.reshape(pair * TILE, wide).astype(jnp.bfloat16)
        return shift_values

    def compute(slots, shift_values, chunk, stats):
        both = jnp.concatenate(
            [fields[which, chunk].reshape(padded_len * TILE, inner_dev) for which in range(2)], axis=1
        )
        product = jnp.dot(expanded[...], both, preferred_element_type=jnp.float32)
        product = product.reshape(pair, TILE, 2 * inner_dev)
        ritz = product[:, :, :inner_dev]
        resid = product[:, :, inner_dev:] - shift_values * ritz
        for kind, cols in enumerate((ritz, resid)):
            squares = jnp.sum(jnp.sum(cols * cols, axis=1), axis=1, keepdims=True)
            stats = jnp.where(lane == 2 * chunk + kind, squares, stats)
            inverse = expand_rows(PEAK / jnp.sqrt(jnp.maximum(squares, LEAST)), inner_dev)
            for index, slot in enumerate(slots):
                part = slice(index * wanted_dev, (index + 1) * wanted_dev)
                if slot == 0:
                    put_out(kind, chunk, grp, cols[part])
                else:
                    coded[slot - 1, chunk, :, kind * inner_dev : (kind + 1) * inner_dev] = encode(
                        cols[part], inverse[part]
                    ).reshape(block, inner_dev).astype(jnp.bfloat16)
        return stats

    def put_out(kind, chunk, source, cols):
        span = pl.ds(pl.multiple_of(chunk * TILE, TILE), TILE)
        lanes = pl.ds(pl.multiple_of(source * inner_dev, inner_dev), inner_dev)
        (ritz_ref, resid_ref)[kind][:, span, lanes] = cols

    def data_copy(mask, chunk):
        return pltpu.make_async_remote_copy(
            src_ref=coded.at[mask - 1, chunk],
            dst_ref=received.at[mask - 1, chunk],
            send_sem=data_sems.at[0, mask - 1, chunk],
            recv_sem=data_sems.at[1, mask - 1, chunk],
            device_id=device(mask, plane, core),
            device_id_type=MESH,
        )

    def stat_copy(mask):
        return pltpu.make_async_remote_copy(
            src_ref=stat_send.at[mask],
            dst_ref=stat_recv.at[mask],
            send_sem=stat_sems.at[0, mask],
            recv_sem=stat_sems.at[1, mask],
            device_id=device(mask, plane, core),
            device_id_type=MESH,
        )

    def square_copy(mask, ahead, flip):
        return pltpu.make_async_remote_copy(
            src_ref=square_send.at[mask],
            dst_ref=square_recv.at[grp * rows + row],
            send_sem=square_sems.at[0, mask, ahead, flip],
            recv_sem=square_sems.at[1, mask, ahead, flip],
            device_id=device(mask, lax.rem(plane + ahead, planes), lax.rem(core + flip, 2)),
            device_id_type=MESH,
        )

    def squares_to(ahead):
        for mask in range(groups):
            for flip in range(2):
                square_copy(mask, ahead, flip).start()

    def near_squares(action):
        for mask in range(groups):
            for flip in range(0 if mask else 1, 2):
                action(square_copy(mask, 0, flip))

    def finish_stats(slots, stats):
        parity = lane & 1
        column = lax.rem(grid_iota((pair, LANES), 0), wanted_dev)
        line = jnp.zeros((pair, LANES), jnp.float32)
        for kind in range(2):
            sums = jnp.sum(jnp.where(parity == kind, stats, 0.0), axis=1, keepdims=True)
            line = jnp.where(lane == column + kind * wanted_dev, sums, line)
        scales = jnp.sqrt(jnp.maximum(stats, LEAST))
        for index, slot in enumerate(slots):
            part = slice(index * wanted_dev, (index + 1) * wanted_dev)
            square_send[slot] = jnp.sum(line[part], axis=0, keepdims=True)
            if slot:
                stat_send[slot] = scales[part]

    nothing = jnp.zeros((pair, LANES), jnp.float32)
    early = plane < cdiv(planes, 2)

    shift_values = prepare((1, 2))

    def first(step, stats):
        for half in range(2):
            chunk = 2 * step + half
            for copy in loads(chunk):
                copy.wait()
            stats = compute((1, 2), shift_values, chunk, stats)
            if half == 0:
                for mask in (1, 2):
                    data_copy(mask, step).start()
        return stats

    stats = lax.fori_loop(0, chunks // 2, first, nothing)
    finish_stats((1, 2), stats)

    coef_wait(3)
    shift_other = prepare((3, 0))

    def second(step, stats):
        for half in range(2):
            stats = compute((3, 0), shift_other, 2 * step + half, stats)
            if half == 0:
                @pl.when(early)
                def _():
                    for mask in (1, 2):
                        data_copy(mask, chunks // 2 + step).start()
        return stats

    stats = lax.fori_loop(0, chunks // 2, second, nothing)
    finish_stats((3, 0), stats)

    for mask in (1, 2, 3):
        stat_copy(mask).start()
    near_squares(lambda copy: copy.start())

    if planes > 1:
        @pl.when(core == 0)
        def _():
            pl.semaphore_wait(barrier, planes - 1)

            def tell(ahead, carry):
                signal(plane_sem.at[plane], device(0, lax.rem(plane + ahead, planes), 0))
                return carry

            lax.fori_loop(1, planes, tell, 0)

    def far_squares(other, carry):
        @pl.when(core == 0)
        def _():
            pl.semaphore_wait(plane_sem.at[other], 1)
            signal(go_sem.at[other], device(0, plane, 1))

        @pl.when(lead)
        def _():
            pl.semaphore_wait(go_sem.at[other], 1)

        squares_to(lax.rem(other + planes - plane, planes))
        return carry

    lax.fori_loop(0, plane, far_squares, 0)

    @pl.when(jnp.logical_not(early))
    def _():
        def rest(chunk, carry):
            for mask in (1, 2):
                data_copy(mask, chunk).start()
            return carry

        lax.fori_loop(chunks // 2, chunks, rest, 0)

    def across(chunk, carry):
        data_copy(3, chunk).start()
        return carry

    lax.fori_loop(0, chunks, across, 0)
    lax.fori_loop(plane + 1, planes, far_squares, 0)

    for mask in (1, 2, 3):
        stat_copy(mask).wait()

    lane_dev = grid_iota((wanted_dev, LANES), 1)

    def take(masks, chunk, carry):
        for mask in masks:
            data_copy(mask, chunk).wait()
            for kind in range(2):
                scale = jnp.sum(
                    jnp.where(lane_dev == 2 * chunk + kind, stat_recv[mask], 0.0), axis=1, keepdims=True
                )
                codes = received[mask - 1, chunk, :, kind * inner_dev : (kind + 1) * inner_dev]
                size = decode(codes.astype(jnp.float32)).reshape(wanted_dev, TILE, inner_dev)
                put_out(kind, chunk, partner(mask), size * expand_rows(scale * (1.0 / PEAK), inner_dev))
        return carry

    lax.fori_loop(0, chunks, functools.partial(take, (1, 2)), 0)
    lax.fori_loop(0, chunks, functools.partial(take, (3,)), 0)

    near_squares(lambda copy: copy.wait())

    def far_wait(ahead, carry):
        for mask in range(groups):
            for flip in range(2):
                square_copy(mask, ahead, flip).wait()
        return carry

    lax.fori_loop(1, planes, far_wait, 0)
    square_recv[grp * rows + row] = square_send[0]
    total_ref[...] = jnp.sum(square_recv[...], axis=0)

    @pl.when(lead)
    def _():
        for copy in own_sends + relay_sends:
            copy.wait_send()


def finish_kernel(rows_total, ritz_in, resid_in, total_ref, ritz_out, resid_out, norm_ref, scaled, sems):
    wanted_dev, outer_dev, inner = ritz_in.shape
    pieces = sems.shape[1]
    several = outer_dev // pieces
    lanes = grid_iota((wanted_dev, LANES), 1)
    columns = grid_iota((wanted_dev, LANES), 0)
    total = jnp.broadcast_to(total_ref[...], (wanted_dev, LANES))
    unit = 1.0 / (SHIFT * SHIFT)

    def pick(lane):
        return jnp.sum(jnp.where(lanes == lane, total, 0.0), axis=1, keepdims=True) * unit

    ritz_squares = pick(columns) + 1.0
    resid_squares = pick(columns + wanted_dev)
    factor = jnp.sqrt(rows_total / ritz_squares)
    spot = expand_rows(factor * (1.0 / SHIFT), inner)
    copies = []
    for piece in range(pieces):
        span = slice(piece * several, (piece + 1) * several)
        for kind, (source, out) in enumerate(((ritz_in, ritz_out), (resid_in, resid_out))):
            scaled[kind, :, span] = source[:, span] * spot
            copy = pltpu.make_async_copy(scaled.at[kind, :, span], out.at[:, span], sems.at[kind, piece])
            copy.start()
            copies.append(copy)
    norms = jnp.broadcast_to(jnp.sqrt(resid_squares / ritz_squares), (wanted_dev, LANES))
    norm_ref[...] = jnp.sum(jnp.where(lanes == columns, norms, 0.0), axis=0)[:wanted_dev]
    for copy in copies:
        copy.wait()


def body(groups, rows, krylov_basis, krylov_image, tridiag_vectors, ritz_values):
    krylov_len, outer_dev, inner_dev = krylov_basis.shape
    wanted_dev = tridiag_vectors.shape[1]
    chunks = outer_dev // TILE
    block = wanted_dev * TILE
    planes = rows // 2
    assert groups == 4 and rows == 2 * planes and chunks % 2 == 0
    padded_len = cdiv(krylov_len, STEP) * STEP
    rows_total = float(outer_dev * inner_dev * groups * rows)
    f32, bf16 = jnp.float32, jnp.bfloat16
    dma, regular = pltpu.SemaphoreType.DMA, pltpu.SemaphoreType.REGULAR
    vmem = pl.BlockSpec(memory_space=pltpu.VMEM)
    hbm = pl.BlockSpec(memory_space=pltpu.HBM)
    parts = cdiv(padded_len, LANES)
    out = jax.ShapeDtypeStruct((wanted_dev, outer_dev, groups * inner_dev), f32)
    ritz, resid, total = pl.pallas_call(
        functools.partial(exchange_kernel, groups, rows),
        name="exchange",
        out_shape=(out, out, jax.ShapeDtypeStruct((1, LANES), f32)),
        in_specs=[hbm] * 4,
        out_specs=(vmem, vmem, vmem),
        scratch_shapes=[
            pltpu.VMEM((groups, wanted_dev, krylov_len), bf16),
            pltpu.VMEM((groups, 1, wanted_dev), bf16),
            pltpu.VMEM((2, chunks, padded_len, TILE, inner_dev), bf16),
            pltpu.VMEM((LANES, LANES * TILE), bf16),
            pltpu.VMEM((parts, 2 * wanted_dev, LANES * TILE), f32),
            pltpu.VMEM((2 * wanted_dev * TILE, padded_len * TILE), bf16),
            pltpu.VMEM((groups - 1, chunks, block, 2 * inner_dev), bf16),
            pltpu.VMEM((groups - 1, chunks, block, 2 * inner_dev), bf16),
            pltpu.VMEM((groups, wanted_dev, LANES), f32),
            pltpu.VMEM((groups, wanted_dev, LANES), f32),
            pltpu.VMEM((groups, 1, LANES), f32),
            pltpu.VMEM((groups * rows, 1, LANES), f32),
            dma((2,)),
            dma((6, 2)),
            dma((groups - 1, 2)),
            dma((2, chunks)),
            dma((2, groups - 1, chunks)),
            dma((2, groups)),
            dma((2, groups, planes, 2)),
            regular,
            regular((planes,)),
            regular((planes,)),
        ],
        compiler_params=pltpu.CompilerParams(
            collective_id=0, has_side_effects=True, vmem_limit_bytes=48 * MIB
        ),
    )(tridiag_vectors.T, ritz_values[None], krylov_basis, krylov_image)
    pieces = math.gcd(chunks, 8)
    return pl.pallas_call(
        functools.partial(finish_kernel, rows_total),
        name="finish",
        out_shape=(out, out, jax.ShapeDtypeStruct((wanted_dev,), f32)),
        in_specs=[vmem] * 3,
        out_specs=(hbm, hbm, vmem),
        scratch_shapes=[
            pltpu.VMEM((2, wanted_dev, outer_dev, groups * inner_dev), f32),
            dma((2, pieces)),
        ],
        compiler_params=pltpu.CompilerParams(vmem_limit_bytes=16 * MIB),
    )(ritz, resid, total)


def solution(mesh):
    placed = (P(None, "row", "grp"), P(None, "row", "grp"), P(None, "grp"), P("grp"))
    return jax.shard_map(
        functools.partial(body, mesh.shape["grp"], mesh.shape["row"]),
        mesh=mesh,
        in_specs=placed,
        out_specs=(P("grp", "row", None), P("grp", "row", None), P("grp")),
        check_vma=False,
    )
```

time: 30.5 us -> 32.7 us (1.072)
  the two profiles are of different devices: /device:TPU:0 before, /device:TPU:25 now
where the time goes in v1:
time: 32.7 us; the launch traced here: 32.5 us
  Pallas kernels  30.5 us (93%)
  local copies, waits for them, and re-layouts  1.34 us (4%)
  between operations  0.65 us (2%)
    pallas_call x1, Pallas kernels, body(): pl.pallas_call(functools.partial(exchange_kernel, groups, rows), name='ex...  28.5 us
    pallas_call x1, Pallas kernels, body(): pl.pallas_call(functools.partial(finish_kernel, rows_total), name='finish...  2.05 us
    unnamed x4, local copies, waits for them, and re-layouts  1.34 us

profile of v1, /device:TPU:25, one launch (start us, length us, event | category | flops | bytes accessed | tf_op | source)
XLA Modules:
  0.0 32.5 jit_solution(5003175007185290984)
XLA Ops:
  0.6 0.0 copy-start
  0.6 0.7 %copy-done = bf16[300,8]{0,1:T(8,128)(2,1)S(1)} copy-done((bf16[300,8]{0,1:T(8,128)(2,1)S(1)}, bf16[300,8]{0,1:T(8,128)(2,1)}, u32[]{:S(2)}) %copy-start) | copy-done | bytes 4824
  1.3 0.0 copy-start.1
  1.3 0.7 %copy-done.1 = bf16[8]{0:T(256)(128)(2,1)S(1)} copy-done((bf16[8]{0:T(256)(128)(2,1)S(1)}, bf16[8]{0:T(256)(128)(2,1)}, u32[]{:S(2)}) %copy-start.1) | copy-done | bytes 40
  2.0 28.5 %exchange.1 = (f32[8,64,512]{2,1,0:T(8,128)S(1)}, f32[8,64,512]{2,1,0:T(8,128)S(1)}, f32[1,128]{1,0:T(1,128)S(1)}) custom-call(bf16[8,300]{1,0:T(8,128)(2,1)S(1)} %bitcast.2, bf16[1,8]{1,0:T(2,128)(2,1)S(1)} %bitcast.3, bf16[300,64,128]{2,1,0:T(8,128)(2,1)} %basis_ref.1, bf16[300,64,128]{2,1,0:T(8,128)(2,1)} %image_ref.1), custom_call_target="tpu_custom_call" | custom-call | tf_op jit(solution)/shard_map/exchange/pallas_call | solution.py:443
  30.5 2.1 %finish.1 = (f32[8,64,512]{2,1,0:T(8,128)}, f32[8,64,512]{2,1,0:T(8,128)}, f32[8]{0:T(128)}) custom-call(f32[8,64,512]{2,1,0:T(8,128)S(1)} %get-tuple-element.6.ritz_in, f32[8,64,512]{2,1,0:T(8,128)S(1)} %get-tuple-element.7.resid_in, f32[1,128]{1,0:T(1,128)S(1)} %get-tuple-element.8.total_ref), custom_call_target="tpu_custom_call" | custom-call | tf_op jit(solution)/shard_map/finish/pallas_call | solution.py:478
Async XLA Ops:
  0.6 0.7 %copy-start = (bf16[300,8]{0,1:T(8,128)(2,1)S(1)}, bf16[300,8]{0,1:T(8,128)(2,1)}, u32[]{:S(2)}) copy-start(bf16[300,8]{0,1:T(8,128)(2,1)} %param.6) | copy-start | bytes 14404
  1.3 0.7 %copy-start.1 = (bf16[8]{0:T(256)(128)(2,1)S(1)}, bf16[8]{0:T(256)(128)(2,1)}, u32[]{:S(2)}) copy-start(bf16[8]{0:T(256)(128)(2,1)} %param.7) | copy-start | bytes 52

commit v2 on v1

v2 whole, which is shorter than its diff:
```python
import functools
import math

import jax
import jax.numpy as jnp
from jax import lax
from jax.experimental import pallas as pl
from jax.experimental.pallas import tpu as pltpu
from jax.sharding import PartitionSpec as P

MESH = pl.DeviceIdType.MESH
MIB = 1 << 20
TILE = 8
STEP = 16
LANES = 128
POWER = 13
PEAK = 2.0 ** (126.0 / POWER)
SHIFT = 2.0**30
LEAST = 1e-36


def cdiv(a, b):
    return (a + b - 1) // b


def grid_iota(shape, dim):
    return lax.broadcasted_iota(jnp.int32, shape, dim)


def expand_rows(cols, width):
    return jnp.broadcast_to(cols, (cols.shape[0], width)).reshape(cols.shape[0], 1, width)


def encode(cols, inverse):
    y = cols * inverse
    y2 = y * y
    y4 = y2 * y2
    y8 = y4 * y4
    return (y8 * y4) * y


def decode(codes):
    size = jnp.exp2(jnp.log(jnp.abs(codes)) * (1.0 / (POWER * math.log(2.0))))
    return jnp.where(codes < 0.0, -size, size)


def exchange_kernel(
    groups, rows,
    tridiag_ref, values_ref, basis_ref, image_ref,
    ritz_ref, resid_ref, total_ref,
    coefs, values, fields, spread, reps, expanded, coded, received,
    stat_send, stat_recv, square_send, square_recv,
    coef_load, coef_send, coef_recv, load_sem, send_sem, recv_sem, small_send, small_recv,
    ready_sem, order_sem,
):
    wanted_dev, krylov_len = tridiag_ref.shape
    chunks = fields.shape[0]
    pairs = chunks // 2
    padded_len = fields.shape[2]
    inner_dev = basis_ref.shape[2]
    steps = padded_len // STEP
    wide = STEP * TILE
    block = wanted_dev * TILE
    planes = rows // 2
    grp = lax.axis_index("grp")
    row = lax.axis_index("row")
    core = lax.rem(row, 2)
    plane = lax.div(row, 2)
    lead = core == 1

    def partner(mask):
        if mask == 0:
            return grp
        if mask == 1:
            return grp + 1 - 2 * lax.rem(grp, 2)
        if mask == 2:
            return lax.rem(grp + 2, groups)
        return groups - 1 - grp

    def device(mask, at_plane, at_core):
        return {"grp": partner(mask), "row": 2 * at_plane + at_core}

    def signal(sem, where):
        pl.semaphore_signal(sem, inc=1, device_id=where, device_id_type=MESH)

    barrier = pltpu.get_barrier_semaphore()
    for mask in (1, 2):
        signal(barrier, device(mask, plane, 1))

    coef_loads = [
        pltpu.make_async_copy(tridiag_ref, coefs.at[0], coef_load.at[0]),
        pltpu.make_async_copy(values_ref, values.at[0], coef_load.at[1]),
    ]
    for copy in coef_loads:
        copy.start()

    @pl.when(core == 0)
    def _():
        signal(barrier, device(0, plane, 1))

        def greet(ahead, carry):
            signal(barrier, device(0, lax.rem(plane + ahead, planes), 0))
            return carry

        lax.fori_loop(1, planes, greet, 0)

    for chunk in range(chunks):
        for which, ref in enumerate((basis_ref, image_ref)):
            pltpu.make_async_copy(
                ref.at[:, chunk * TILE : (chunk + 1) * TILE, :],
                fields.at[chunk, which, pl.ds(0, krylov_len)],
                load_sem.at[chunk // 2],
            ).start()

    def land(ref, sem):
        pltpu.make_async_copy(ref, ref, sem).wait()

    def load_wait(step):
        land(fields.at[pl.ds(2 * step, 2), :, pl.ds(0, krylov_len)], load_sem.at[step])

    if padded_len > krylov_len:
        for chunk in range(chunks):
            for which in range(2):
                fields[chunk, which, pl.ds(krylov_len, padded_len - krylov_len)] = jnp.zeros(
                    (padded_len - krylov_len, TILE, inner_dev), jnp.bfloat16
                )
    shape = spread.shape
    spread[...] = jnp.where(
        lax.shift_right_logical(grid_iota(shape, 1), 3) == grid_iota(shape, 0), SHIFT, 0.0
    ).astype(jnp.bfloat16)

    for copy in coef_loads:
        copy.wait()

    def coef_copies(source, slot, mask, at_core):
        return [
            pltpu.make_async_remote_copy(
                src_ref=ref.at[source],
                dst_ref=ref.at[slot],
                send_sem=coef_send.at[kind],
                recv_sem=coef_recv.at[slot - 1, kind],
                device_id=device(mask, plane, at_core),
                device_id_type=MESH,
            )
            for kind, ref in enumerate((coefs, values))
        ]

    own_sends = [
        copy
        for mask in (1, 2)
        for at_core in (1, 0)
        for copy in coef_copies(0, mask, mask, at_core)
    ]
    relay_sends = [copy for at_core in (1, 0) for copy in coef_copies(1, 3, 2, at_core)]

    def coef_wait(slot):
        for copy in coef_copies(0, slot, 1, 1):
            copy.wait_recv()

    @pl.when(lead)
    def _():
        pl.semaphore_wait(barrier, 5)
        for copy in own_sends:
            copy.start()
        signal(ready_sem, device(0, plane, 0))
        coef_wait(1)
        for copy in relay_sends:
            copy.start()
        coef_wait(2)

    @pl.when(core == 0)
    def _():
        pl.semaphore_wait(ready_sem, 1)
        coef_wait(1)
        coef_wait(2)

    near = grid_iota((wanted_dev, wanted_dev), 0) == grid_iota((wanted_dev, wanted_dev), 1)
    same = (grid_iota((TILE, wide), 1) & (TILE - 1)) == grid_iota((TILE, wide), 0)
    per_part = LANES // STEP
    pair = 2 * wanted_dev
    lane = grid_iota((pair, LANES), 1)

    def prepare(slots):
        shifts = []
        for slot in slots:
            spot = jnp.broadcast_to(values[slot].astype(jnp.float32), (wanted_dev, wanted_dev))
            shifts.append(jnp.sum(jnp.where(near, spot, 0.0), axis=1, keepdims=True))
        shift_values = expand_rows(jnp.concatenate(shifts, axis=0), inner_dev)
        both = jnp.concatenate([coefs[slot] for slot in slots], axis=0)
        for part in range(cdiv(krylov_len, LANES)):
            piece = both[:, part * LANES : min((part + 1) * LANES, krylov_len)]
            reps[part] = jnp.dot(piece, spread[: piece.shape[1]], preferred_element_type=jnp.float32)
        for step in range(steps):
            at = (step % per_part) * wide
            spot = reps[step // per_part, :, at : at + wide]
            spot = jnp.where(same[None], spot.reshape(pair, 1, wide), 0.0)
            expanded[:, step * wide : (step + 1) * wide] = spot.reshape(pair * TILE, wide).astype(jnp.bfloat16)
        return shift_values

    def compute(slots, shift_values, step, stats):
        both = jnp.concatenate(
            [
                fields[2 * step + half, which].reshape(padded_len * TILE, inner_dev)
                for half in range(2)
                for which in range(2)
            ],
            axis=1,
        )
        product = jnp.dot(expanded[...], both, preferred_element_type=jnp.float32)
        product = product.reshape(pair, TILE, 4 * inner_dev)
        for half in range(2):
            chunk = 2 * step + half
            at = 2 * half * inner_dev
            ritz = product[:, :, at : at + inner_dev]
            resid = product[:, :, at + inner_dev : at + 2 * inner_dev] - shift_values * ritz
            for kind, cols in enumerate((ritz, resid)):
                squares = jnp.sum(jnp.sum(cols * cols, axis=1), axis=1, keepdims=True)
                stats = jnp.where(lane == 2 * chunk + kind, squares, stats)
                inverse = expand_rows(PEAK / jnp.sqrt(jnp.maximum(squares, LEAST)), inner_dev)
                for index, slot in enumerate(slots):
                    part = slice(index * wanted_dev, (index + 1) * wanted_dev)
                    if slot == 0:
                        put_out(kind, chunk, grp, cols[part])
                    else:
                        coded[slot - 1, chunk, :, kind * inner_dev : (kind + 1) * inner_dev] = encode(
                            cols[part], inverse[part]
                        ).reshape(block, inner_dev).astype(jnp.bfloat16)
        return stats

    def put_out(kind, chunk, source, cols):
        span = pl.ds(pl.multiple_of(chunk * TILE, TILE), TILE)
        lanes = pl.ds(pl.multiple_of(source * inner_dev, inner_dev), inner_dev)
        (ritz_ref, resid_ref)[kind][:, span, lanes] = cols

    def data_copy(mask, step):
        span = pl.ds(2 * step, 2)
        return pltpu.make_async_remote_copy(
            src_ref=coded.at[mask - 1, span],
            dst_ref=received.at[mask - 1, span],
            send_sem=send_sem,
            recv_sem=recv_sem.at[0 if mask < 3 else 1, step],
            device_id=device(mask, plane, core),
            device_id_type=MESH,
        )

    def stat_copy(mask):
        return pltpu.make_async_remote_copy(
            src_ref=stat_send.at[mask],
            dst_ref=stat_recv.at[mask],
            send_sem=small_send.at[0],
            recv_sem=small_recv.at[0],
            device_id=device(mask, plane, core),
            device_id_type=MESH,
        )

    def squares_to(mask, at_plane, flip):
        pltpu.make_async_remote_copy(
            src_ref=square_send.at[mask],
            dst_ref=square_recv.at[grp * rows + row],
            send_sem=small_send.at[1],
            recv_sem=small_recv.at[1],
            device_id=device(mask, at_plane, lax.rem(core + flip, 2)),
            device_id_type=MESH,
        ).start()

    def far_squares(at_plane, carry):
        for mask in range(groups):
            for flip in range(2):
                squares_to(mask, at_plane, flip)
        return carry

    def agree(side, count):
        @pl.when(core == 0)
        def _():
            pl.semaphore_wait(order_sem.at[side], count)
            signal(order_sem.at[side], device(0, plane, 1))

        @pl.when(lead)
        def _():
            pl.semaphore_wait(order_sem.at[side], 1)

    def finish_stats(slots, stats):
        parity = lane & 1
        column = lax.rem(grid_iota((pair, LANES), 0), wanted_dev)
        line = jnp.zeros((pair, LANES), jnp.float32)
        for kind in range(2):
            sums = jnp.sum(jnp.where(parity == kind, stats, 0.0), axis=1, keepdims=True)
            line = jnp.where(lane == column + kind * wanted_dev, sums, line)
        scales = jnp.sqrt(jnp.maximum(stats, LEAST))
        for index, slot in enumerate(slots):
            part = slice(index * wanted_dev, (index + 1) * wanted_dev)
            square_send[slot] = jnp.sum(line[part], axis=0, keepdims=True)
            if slot:
                stat_send[slot] = scales[part]

    nothing = jnp.zeros((pair, LANES), jnp.float32)
    early = plane == 0

    shift_values = prepare((1, 2))

    def first(step, stats):
        load_wait(step)
        stats = compute((1, 2), shift_values, step, stats)
        for mask in (1, 2):
            data_copy(mask, step).start()
        return stats

    stats = lax.fori_loop(0, pairs, first, nothing)
    finish_stats((1, 2), stats)

    coef_wait(3)
    if planes > 1:
        @pl.when(core == 0)
        def _():
            pl.semaphore_wait(barrier, planes - 1)

            def lower(other, carry):
                signal(order_sem.at[1], device(0, other, 0))
                return carry

            def upper(other, carry):
                signal(order_sem.at[0], device(0, other, 0))
                return carry

            lax.fori_loop(plane + 1, planes, upper, 0)
            lax.fori_loop(0, plane, lower, 0)

    shift_other = prepare((3, 0))

    def second(step, stats):
        stats = compute((3, 0), shift_other, step, stats)

        @pl.when(jnp.logical_and(early, lax.rem(step, 2) == 1))
        def _():
            data_copy(3, lax.div(step, 2)).start()

        return stats

    stats = lax.fori_loop(0, pairs, second, nothing)
    finish_stats((3, 0), stats)

    for mask in (1, 2, 3):
        stat_copy(mask).start()
    for mask in range(groups):
        for flip in range(0 if mask else 1, 2):
            squares_to(mask, plane, flip)
    if planes > 1:
        @pl.when(plane > 0)
        def _():
            agree(0, plane)
            lax.fori_loop(0, plane, far_squares, 0)

    def across(step, carry):
        data_copy(3, step).start()
        return carry

    lax.fori_loop(jnp.where(early, pairs // 2, 0), pairs, across, 0)

    land(stat_recv.at[pl.ds(1, groups - 1)], small_recv.at[0])

    lane_dev = grid_iota((wanted_dev, LANES), 1)

    def take(masks, step, carry):
        land(
            received.at[pl.ds(masks[0] - 1, len(masks)), pl.ds(2 * step, 2)],
            recv_sem.at[0 if masks[0] < 3 else 1, step],
        )
        for half in range(2):
            chunk = 2 * step + half
            for mask in masks:
                for kind in range(2):
                    scale = jnp.sum(
                        jnp.where(lane_dev == 2 * chunk + kind, stat_recv[mask], 0.0), axis=1, keepdims=True
                    )
                    codes = received[mask - 1, chunk, :, kind * inner_dev : (kind + 1) * inner_dev]
                    size = decode(codes.astype(jnp.float32)).reshape(wanted_dev, TILE, inner_dev)
                    put_out(kind, chunk, partner(mask), size * expand_rows(scale * (1.0 / PEAK), inner_dev))
        return carry

    lax.fori_loop(0, pairs, functools.partial(take, (1, 2)), 0)
    if planes > 1:
        @pl.when(plane < planes - 1)
        def _():
            agree(1, planes - 1 - plane)
            lax.fori_loop(plane + 1, planes, far_squares, 0)

    lax.fori_loop(0, pairs, functools.partial(take, (3,)), 0)

    others = groups * rows - 1
    land(square_recv.at[pl.ds(0, others)], small_recv.at[1])
    land(square_recv.at[pl.ds(0, others)], small_send.at[1])
    land(stat_send.at[pl.ds(1, groups - 1)], small_send.at[0])
    land(coded, send_sem)
    square_recv[grp * rows + row] = square_send[0]
    total_ref[...] = jnp.sum(square_recv[...], axis=0)

    @pl.when(lead)
    def _():
        for kind, ref in enumerate((coefs, values)):
            land(ref, coef_send.at[kind])


def finish_kernel(rows_total, ritz_in, resid_in, total_ref, ritz_out, resid_out, norm_ref, scaled, sems):
    wanted_dev, outer_dev, inner = ritz_in.shape
    pieces = math.gcd(outer_dev // TILE, 8)
    several = outer_dev // pieces
    lanes = grid_iota((wanted_dev, LANES), 1)
    columns = grid_iota((wanted_dev, LANES), 0)
    total = jnp.broadcast_to(total_ref[...], (wanted_dev, LANES))
    unit = 1.0 / (SHIFT * SHIFT)

    def pick(lane):
        return jnp.sum(jnp.where(lanes == lane, total, 0.0), axis=1, keepdims=True) * unit

    ritz_squares = pick(columns) + 1.0
    resid_squares = pick(columns + wanted_dev)
    factor = jnp.sqrt(rows_total / ritz_squares)
    spot = expand_rows(factor * (1.0 / SHIFT), inner)
    for piece in range(pieces):
        span = slice(piece * several, (piece + 1) * several)
        for kind, (source, out) in enumerate(((ritz_in, ritz_out), (resid_in, resid_out))):
            scaled[kind, :, span] = source[:, span] * spot
            copy = pltpu.make_async_copy(scaled.at[kind, :, span], out.at[:, span], sems.at[kind])
            copy.start()
    norms = jnp.broadcast_to(jnp.sqrt(resid_squares / ritz_squares), (wanted_dev, LANES))
    norm_ref[...] = jnp.sum(jnp.where(lanes == columns, norms, 0.0), axis=0)[:wanted_dev]
    for kind, out in enumerate((ritz_out, resid_out)):
        pltpu.make_async_copy(scaled.at[kind], out, sems.at[kind]).wait()


def body(groups, rows, krylov_basis, krylov_image, tridiag_vectors, ritz_values):
    krylov_len, outer_dev, inner_dev = krylov_basis.shape
    wanted_dev = tridiag_vectors.shape[1]
    chunks = outer_dev // TILE
    block = wanted_dev * TILE
    planes = rows // 2
    assert groups == 4 and rows == 2 * planes and chunks % 2 == 0
    padded_len = cdiv(krylov_len, STEP) * STEP
    rows_total = float(outer_dev * inner_dev * groups * rows)
    f32, bf16 = jnp.float32, jnp.bfloat16
    dma, regular = pltpu.SemaphoreType.DMA, pltpu.SemaphoreType.REGULAR
    vmem = pl.BlockSpec(memory_space=pltpu.VMEM)
    hbm = pl.BlockSpec(memory_space=pltpu.HBM)
    parts = cdiv(padded_len, LANES)
    out = jax.ShapeDtypeStruct((wanted_dev, outer_dev, groups * inner_dev), f32)
    ritz, resid, total = pl.pallas_call(
        functools.partial(exchange_kernel, groups, rows),
        name="exchange",
        out_shape=(out, out, jax.ShapeDtypeStruct((1, LANES), f32)),
        in_specs=[hbm] * 4,
        out_specs=(vmem, vmem, vmem),
        scratch_shapes=[
            pltpu.VMEM((6, wanted_dev, krylov_len), bf16),
            pltpu.VMEM((6, 1, wanted_dev), bf16),
            pltpu.VMEM((chunks, 2, padded_len, TILE, inner_dev), bf16),
            pltpu.VMEM((LANES, LANES * TILE), bf16),
            pltpu.VMEM((parts, 2 * wanted_dev, LANES * TILE), f32),
            pltpu.VMEM((2 * wanted_dev * TILE, padded_len * TILE), bf16),
            pltpu.VMEM((groups - 1, chunks, block, 2 * inner_dev), bf16),
            pltpu.VMEM((groups - 1, chunks, block, 2 * inner_dev), bf16),
            pltpu.VMEM((groups, wanted_dev, LANES), f32),
            pltpu.VMEM((groups, wanted_dev, LANES), f32),
            pltpu.VMEM((groups, 1, LANES), f32),
            pltpu.VMEM((groups * rows, 1, LANES), f32),
            dma((2,)),
            dma((2,)),
            dma((groups - 1, 2)),
            dma((chunks // 2,)),
            dma,
            dma((2, chunks // 2)),
            dma((2,)),
            dma((2,)),
            regular,
            regular((2,)),
        ],
        compiler_params=pltpu.CompilerParams(
            collective_id=0, has_side_effects=True, vmem_limit_bytes=48 * MIB
        ),
    )(*[pltpu.with_memory_space_constraint(x, pltpu.HBM) for x in (tridiag_vectors.T, ritz_values[None])], krylov_basis, krylov_image)
    return pl.pallas_call(
        functools.partial(finish_kernel, rows_total),
        name="finish",
        out_shape=(out, out, jax.ShapeDtypeStruct((wanted_dev,), f32)),
        in_specs=[vmem] * 3,
        out_specs=(hbm, hbm, vmem),
        scratch_shapes=[
            pltpu.VMEM((2, wanted_dev, outer_dev, groups * inner_dev), f32),
            dma((2,)),
        ],
        compiler_params=pltpu.CompilerParams(vmem_limit_bytes=16 * MIB),
    )(ritz, resid, total)


def solution(mesh):
    placed = (P(None, "row", "grp"), P(None, "row", "grp"), P(None, "grp"), P("grp"))
    return jax.shard_map(
        functools.partial(body, mesh.shape["grp"], mesh.shape["row"]),
        mesh=mesh,
        in_specs=placed,
        out_specs=(P("grp", "row", None), P("grp", "row", None), P("grp")),
        check_vma=False,
    )
```

time: 32.7 us -> 23.8 us (0.73)
  the two profiles are of different devices: /device:TPU:25 before, /device:TPU:0 now
where the time goes in v2:
time: 23.8 us; the launch traced here: 23.6 us
  Pallas kernels  23 us (97%)
  between operations  0.64 us (3%)
    pallas_call x1, Pallas kernels, body(): pl.pallas_call(functools.partial(exchange_kernel, groups, rows), name='ex...  21.1 us
    pallas_call x1, Pallas kernels, body(): pl.pallas_call(functools.partial(finish_kernel, rows_total), name='finish...  1.93 us

profile of v2, /device:TPU:0, one launch (start us, length us, event | category | flops | bytes accessed | tf_op | source)
XLA Modules:
  0.0 23.6 jit_solution(11885959451766160204)
XLA Ops:
  0.6 21.1 %exchange.1 = (f32[8,64,512]{2,1,0:T(8,128)S(1)}, f32[8,64,512]{2,1,0:T(8,128)S(1)}, f32[1,128]{1,0:T(1,128)S(1)}) custom-call(bf16[8,300]{1,0:T(8,128)(2,1)} %bitcast.2, bf16[1,8]{1,0:T(2,128)(2,1)} %bitcast.3, bf16[300,64,128]{2,1,0:T(8,128)(2,1)} %basis_ref.1, bf16[300,64,128]{2,1,0:T(8,128)(2,1)} %image_ref.1), custom_call_target="tpu_custom_call" | custom-call | tf_op jit(solution)/shard_map/exchange/pallas_call | solution.py:446
  21.7 1.9 %finish.1 = (f32[8,64,512]{2,1,0:T(8,128)}, f32[8,64,512]{2,1,0:T(8,128)}, f32[8]{0:T(128)}) custom-call(f32[8,64,512]{2,1,0:T(8,128)S(1)} %get-tuple-element.6.ritz_in, f32[8,64,512]{2,1,0:T(8,128)S(1)} %get-tuple-element.7.resid_in, f32[1,128]{1,0:T(1,128)S(1)} %get-tuple-element.8.total_ref), custom_call_target="tpu_custom_call" | custom-call | tf_op jit(solution)/shard_map/finish/pallas_call | solution.py:480

commit v3 on v2

--- a/solution.py
+++ b/solution.py
@@ -45,10 +45,10 @@
 
 
 def exchange_kernel(
-    groups, rows,
+    groups, rows, rows_total,
     tridiag_ref, values_ref, basis_ref, image_ref,
-    ritz_ref, resid_ref, total_ref,
-    coefs, values, fields, spread, reps, expanded, coded, received,
+    ritz_ref, resid_ref, factor_ref, norm_ref,
+    coefs, values, fields, spread, expanded, coded, received,
     stat_send, stat_recv, square_send, square_recv,
     coef_load, coef_send, coef_recv, load_sem, send_sem, recv_sem, small_send, small_recv,
     ready_sem, order_sem,
@@ -189,28 +189,27 @@
         both = jnp.concatenate([coefs[slot] for slot in slots], axis=0)
         for part in range(cdiv(krylov_len, LANES)):
             piece = both[:, part * LANES : min((part + 1) * LANES, krylov_len)]
-            reps[part] = jnp.dot(piece, spread[: piece.shape[1]], preferred_element_type=jnp.float32)
-        for step in range(steps):
-            at = (step % per_part) * wide
-            spot = reps[step // per_part, :, at : at + wide]
-            spot = jnp.where(same[None], spot.reshape(pair, 1, wide), 0.0)
-            expanded[:, step * wide : (step + 1) * wide] = spot.reshape(pair * TILE, wide).astype(jnp.bfloat16)
+            wider = jnp.dot(piece, spread[: piece.shape[1]], preferred_element_type=jnp.float32)
+            for step in range(part * per_part, min((part + 1) * per_part, steps)):
+                at = (step % per_part) * wide
+                spot = jnp.where(same[None], wider[:, at : at + wide].reshape(pair, 1, wide), 0.0)
+                expanded[:, step * wide : (step + 1) * wide] = spot.reshape(pair * TILE, wide).astype(jnp.bfloat16)
         return shift_values
 
-    def compute(slots, shift_values, step, stats):
+    def compute(slots, shift_values, start, count, stats):
         both = jnp.concatenate(
             [
-                fields[2 * step + half, which].reshape(padded_len * TILE, inner_dev)
-                for half in range(2)
+                fields[start + more, which].reshape(padded_len * TILE, inner_dev)
+                for more in range(count)
                 for which in range(2)
             ],
             axis=1,
         )
         product = jnp.dot(expanded[...], both, preferred_element_type=jnp.float32)
-        product = product.reshape(pair, TILE, 4 * inner_dev)
-        for half in range(2):
-            chunk = 2 * step + half
-            at = 2 * half * inner_dev
+        product = product.reshape(pair, TILE, 2 * count * inner_dev)
+        for more in range(count):
+            chunk = start + more
+            at = 2 * more * inner_dev
             ritz = product[:, :, at : at + inner_dev]
             resid = product[:, :, at + inner_dev : at + 2 * inner_dev] - shift_values * ritz
             for kind, cols in enumerate((ritz, resid)):
@@ -232,13 +231,13 @@
         lanes = pl.ds(pl.multiple_of(source * inner_dev, inner_dev), inner_dev)
         (ritz_ref, resid_ref)[kind][:, span, lanes] = cols
 
-    def data_copy(mask, step):
-        span = pl.ds(2 * step, 2)
+    def data_copy(mask, start, count=2):
+        span = pl.ds(start, count)
         return pltpu.make_async_remote_copy(
             src_ref=coded.at[mask - 1, span],
             dst_ref=received.at[mask - 1, span],
             send_sem=send_sem,
-            recv_sem=recv_sem.at[0 if mask < 3 else 1, step],
+            recv_sem=recv_sem.at[mask - 1, lax.div(start, 2)],
             device_id=device(mask, plane, core),
             device_id_type=MESH,
         )
@@ -248,7 +247,7 @@
             src_ref=stat_send.at[mask],
             dst_ref=stat_recv.at[mask],
             send_sem=small_send.at[0],
-            recv_sem=small_recv.at[0],
+            recv_sem=small_recv.at[0 if mask < 3 else 2],
             device_id=device(mask, plane, core),
             device_id_type=MESH,
         )
@@ -294,19 +293,22 @@
                 stat_send[slot] = scales[part]
 
     nothing = jnp.zeros((pair, LANES), jnp.float32)
-    early = plane == 0
-
     shift_values = prepare((1, 2))
-
     def first(step, stats):
         load_wait(step)
-        stats = compute((1, 2), shift_values, step, stats)
-        for mask in (1, 2):
-            data_copy(mask, step).start()
+        stats = compute((1, 2), shift_values, 2 * step, 2, stats)
+        @pl.when(step < pairs - 1)
+        def _():
+            for mask in (1, 2):
+                data_copy(mask, 2 * step).start()
+
         return stats
 
     stats = lax.fori_loop(0, pairs, first, nothing)
     finish_stats((1, 2), stats)
+    for mask in (1, 2):
+        stat_copy(mask).start()
+    data_copy(2, chunks - 2).start()
 
     coef_wait(3)
     if planes > 1:
@@ -328,19 +330,18 @@
     shift_other = prepare((3, 0))
 
     def second(step, stats):
-        stats = compute((3, 0), shift_other, step, stats)
-
-        @pl.when(jnp.logical_and(early, lax.rem(step, 2) == 1))
-        def _():
-            data_copy(3, lax.div(step, 2)).start()
+        stats = compute((3, 0), shift_other, 2 * step, 2, stats)
+
+        @pl.when(lax.rem(step, 2) == 0)
+        def _():
+            data_copy(3, step).start()
 
         return stats
 
     stats = lax.fori_loop(0, pairs, second, nothing)
     finish_stats((3, 0), stats)
 
-    for mask in (1, 2, 3):
-        stat_copy(mask).start()
+    stat_copy(3).start()
     for mask in range(groups):
         for flip in range(0 if mask else 1, 2):
             squares_to(mask, plane, flip)
@@ -351,20 +352,25 @@
             lax.fori_loop(0, plane, far_squares, 0)
 
     def across(step, carry):
-        data_copy(3, step).start()
+        data_copy(3, 2 * step).start()
         return carry
 
-    lax.fori_loop(jnp.where(early, pairs // 2, 0), pairs, across, 0)
-
-    land(stat_recv.at[pl.ds(1, groups - 1)], small_recv.at[0])
+    lax.fori_loop(cdiv(pairs, 2), pairs, across, 0)
+    data_copy(1, chunks - 2).start()
+
+    if planes > 1:
+        @pl.when(plane < planes - 1)
+        def _():
+            agree(1, planes - 1 - plane)
+            lax.fori_loop(plane + 1, planes, far_squares, 0)
+
+    land(stat_recv.at[pl.ds(1, 2)], small_recv.at[0])
 
     lane_dev = grid_iota((wanted_dev, LANES), 1)
 
     def take(masks, step, carry):
-        land(
-            received.at[pl.ds(masks[0] - 1, len(masks)), pl.ds(2 * step, 2)],
-            recv_sem.at[0 if masks[0] < 3 else 1, step],
-        )
+        for mask in masks:
+            land(received.at[mask - 1, pl.ds(2 * step, 2)], recv_sem.at[mask - 1, step])
         for half in range(2):
             chunk = 2 * step + half
             for mask in masks:
@@ -377,53 +383,54 @@
                     put_out(kind, chunk, partner(mask), size * expand_rows(scale * (1.0 / PEAK), inner_dev))
         return carry
 
-    lax.fori_loop(0, pairs, functools.partial(take, (1, 2)), 0)
-    if planes > 1:
-        @pl.when(plane < planes - 1)
-        def _():
-            agree(1, planes - 1 - plane)
-            lax.fori_loop(plane + 1, planes, far_squares, 0)
-
+    lax.fori_loop(0, pairs - 1, functools.partial(take, (1, 2)), 0)
+    take((2,), pairs - 1, 0)
+    land(stat_recv.at[3], small_recv.at[2])
     lax.fori_loop(0, pairs, functools.partial(take, (3,)), 0)
 
     others = groups * rows - 1
     land(square_recv.at[pl.ds(0, others)], small_recv.at[1])
+    square_recv[grp * rows + row] = square_send[0]
+    total = jnp.broadcast_to(jnp.sum(square_recv[...], axis=0), (wanted_dev, LANES))
+    column = grid_iota((wanted_dev, LANES), 0)
+    unit = 1.0 / (SHIFT * SHIFT)
+    ritz_squares, resid_squares = (
+        jnp.sum(jnp.where(lane_dev == column + kind * wanted_dev, total, 0.0), axis=1, keepdims=True) * unit
+        for kind in range(2)
+    )
+    ritz_squares = ritz_squares + 1.0
+    factor_ref[...] = jnp.broadcast_to(
+        jnp.sqrt(rows_total / ritz_squares) * (1.0 / SHIFT), (wanted_dev, LANES)
+    )
+    norms = jnp.broadcast_to(jnp.sqrt(resid_squares / ritz_squares), (wanted_dev, LANES))
+    norm_ref[...] = jnp.sum(jnp.where(lane_dev == column, norms, 0.0), axis=0, keepdims=True)
+
     land(square_recv.at[pl.ds(0, others)], small_send.at[1])
     land(stat_send.at[pl.ds(1, groups - 1)], small_send.at[0])
-    land(coded, send_sem)
-    square_recv[grp * rows + row] = square_send[0]
-    total_ref[...] = jnp.sum(square_recv[...], axis=0)
 
     @pl.when(lead)
     def _():
         for kind, ref in enumerate((coefs, values)):
             land(ref, coef_send.at[kind])
 
-
-def finish_kernel(rows_total, ritz_in, resid_in, total_ref, ritz_out, resid_out, norm_ref, scaled, sems):
-    wanted_dev, outer_dev, inner = ritz_in.shape
-    pieces = math.gcd(outer_dev // TILE, 8)
-    several = outer_dev // pieces
-    lanes = grid_iota((wanted_dev, LANES), 1)
-    columns = grid_iota((wanted_dev, LANES), 0)
-    total = jnp.broadcast_to(total_ref[...], (wanted_dev, LANES))
-    unit = 1.0 / (SHIFT * SHIFT)
-
-    def pick(lane):
-        return jnp.sum(jnp.where(lanes == lane, total, 0.0), axis=1, keepdims=True) * unit
-
-    ritz_squares = pick(columns) + 1.0
-    resid_squares = pick(columns + wanted_dev)
-    factor = jnp.sqrt(rows_total / ritz_squares)
-    spot = expand_rows(factor * (1.0 / SHIFT), inner)
-    for piece in range(pieces):
-        span = slice(piece * several, (piece + 1) * several)
+    take((1,), pairs - 1, 0)
+    land(coded, send_sem)
+
+
+def finish_kernel(ritz_in, resid_in, factor_ref, norm_in, ritz_out, resid_out, norm_out, scaled, norm, sems):
+    wanted_dev, _, inner = ritz_in.shape
+    norm[...] = norm_in[0, :wanted_dev]
+    norm_copy = pltpu.make_async_copy(norm, norm_out, sems.at[2])
+    norm_copy.start()
+    for column in range(wanted_dev):
+        span = slice(column, column + 1)
+        spot = jnp.broadcast_to(factor_ref[span], (TILE, LANES))
+        spot = jnp.concatenate([spot] * (inner // LANES), axis=1)[None]
         for kind, (source, out) in enumerate(((ritz_in, ritz_out), (resid_in, resid_out))):
-            scaled[kind, :, span] = source[:, span] * spot
-            copy = pltpu.make_async_copy(scaled.at[kind, :, span], out.at[:, span], sems.at[kind])
-            copy.start()
-    norms = jnp.broadcast_to(jnp.sqrt(resid_squares / ritz_squares), (wanted_dev, LANES))
-    norm_ref[...] = jnp.sum(jnp.where(lanes == columns, norms, 0.0), axis=0)[:wanted_dev]
+            for at in range(0, source.shape[1], TILE):
+                scaled[kind, span, at : at + TILE] = source[span, at : at + TILE] * spot
+            pltpu.make_async_copy(scaled.at[kind, span], out.at[span], sems.at[kind]).start()
+    norm_copy.wait()
     for kind, out in enumerate((ritz_out, resid_out)):
         pltpu.make_async_copy(scaled.at[kind], out, sems.at[kind]).wait()
 
@@ -441,20 +448,20 @@
     dma, regular = pltpu.SemaphoreType.DMA, pltpu.SemaphoreType.REGULAR
     vmem = pl.BlockSpec(memory_space=pltpu.VMEM)
     hbm = pl.BlockSpec(memory_space=pltpu.HBM)
-    parts = cdiv(padded_len, LANES)
     out = jax.ShapeDtypeStruct((wanted_dev, outer_dev, groups * inner_dev), f32)
-    ritz, resid, total = pl.pallas_call(
-        functools.partial(exchange_kernel, groups, rows),
+    ritz, resid, factor, norms = pl.pallas_call(
+        functools.partial(exchange_kernel, groups, rows, rows_total),
         name="exchange",
-        out_shape=(out, out, jax.ShapeDtypeStruct((1, LANES), f32)),
+        out_shape=(
+            out, out, jax.ShapeDtypeStruct((wanted_dev, LANES), f32), jax.ShapeDtypeStruct((1, LANES), f32),
+        ),
         in_specs=[hbm] * 4,
-        out_specs=(vmem, vmem, vmem),
+        out_specs=(vmem,) * 4,
         scratch_shapes=[
             pltpu.VMEM((6, wanted_dev, krylov_len), bf16),
             pltpu.VMEM((6, 1, wanted_dev), bf16),
             pltpu.VMEM((chunks, 2, padded_len, TILE, inner_dev), bf16),
             pltpu.VMEM((LANES, LANES * TILE), bf16),
-            pltpu.VMEM((parts, 2 * wanted_dev, LANES * TILE), f32),
             pltpu.VMEM((2 * wanted_dev * TILE, padded_len * TILE), bf16),
             pltpu.VMEM((groups - 1, chunks, block, 2 * inner_dev), bf16),
             pltpu.VMEM((groups - 1, chunks, block, 2 * inner_dev), bf16),
@@ -467,9 +474,9 @@
             dma((groups - 1, 2)),
             dma((chunks // 2,)),
             dma,
-            dma((2, chunks // 2)),
+            dma((groups - 1, chunks // 2)),
             dma((2,)),
-            dma((2,)),
+            dma((3,)),
             regular,
             regular((2,)),
         ],
@@ -478,17 +485,18 @@
         ),
     )(*[pltpu.with_memory_space_constraint(x, pltpu.HBM) for x in (tridiag_vectors.T, ritz_values[None])], krylov_basis, krylov_image)
     return pl.pallas_call(
-        functools.partial(finish_kernel, rows_total),
+        finish_kernel,
         name="finish",
         out_shape=(out, out, jax.ShapeDtypeStruct((wanted_dev,), f32)),
-        in_specs=[vmem] * 3,
-        out_specs=(hbm, hbm, vmem),
+        in_specs=[vmem] * 4,
+        out_specs=(hbm, hbm, hbm),
         scratch_shapes=[
             pltpu.VMEM((2, wanted_dev, outer_dev, groups * inner_dev), f32),
-            dma((2,)),
+            pltpu.VMEM((wanted_dev,), f32),
+            dma((3,)),
         ],
         compiler_params=pltpu.CompilerParams(vmem_limit_bytes=16 * MIB),
-    )(ritz, resid, total)
+    )(ritz, resid, factor, norms)
 
 
 def solution(mesh):

time: 23.8 us -> 22.8 us (0.958)
  Pallas kernels: 23 us -> 22 us
    pallas_call x2, Pallas kernels: 23 us -> 22 us  [the longest x1 20.7 us: body(): pl.pallas_call(functools.partial(exchange_kernel, groups, rows, rows_tota...]
where the time goes in v3:
time: 22.8 us; the launch traced here: 22.6 us
  Pallas kernels  22 us (96%)
  between operations  0.64 us (3%)
    pallas_call x1, Pallas kernels, body(): pl.pallas_call(functools.partial(exchange_kernel, groups, rows, rows_tota...  20.7 us
    pallas_call x1, Pallas kernels, body(): pl.pallas_call(finish_kernel, name='finish', out_shape=(out, out, jax.Sha...  1.33 us

profile of v3, /device:TPU:0, one launch (start us, length us, event | category | flops | bytes accessed | tf_op | source)
XLA Modules:
  0.0 22.6 jit_solution(10554340155497179242)
XLA Ops:
  0.6 20.7 %exchange.1 = (f32[8,64,512]{2,1,0:T(8,128)S(1)}, f32[8,64,512]{2,1,0:T(8,128)S(1)}, f32[8,128]{1,0:T(8,128)S(1)}, f32[1,128]{1,0:T(1,128)S(1)}) custom-call(bf16[8,300]{1,0:T(8,128)(2,1)} %bitcast.2, bf16[1,8]{1,0:T(2,128)(2,1)} %bitcast.3, bf16[300,64,128]{2,1,0:T(8,128)(2,1)} %basis_ref.1, bf16[300,64,128]{2,1,0:T(8,128)(2,1)} %image_ref.1), custom_call_target="tpu_custom_call" | custom-call | tf_op jit(solution)/shard_map/exchange/pallas_call | solution.py:452
  21.3 1.3 %finish.1 = (f32[8,64,512]{2,1,0:T(8,128)}, f32[8,64,512]{2,1,0:T(8,128)}, f32[8]{0:T(128)}) custom-call(f32[8,64,512]{2,1,0:T(8,128)S(1)} %get-tuple-element.7.ritz_in, f32[8,64,512]{2,1,0:T(8,128)S(1)} %get-tuple-element.8.resid_in, f32[8,128]{1,0:T(8,128)S(1)} %get-tuple-element.9.factor_ref, f32[1,128]{1,0:T(1,128)S(1)} %get-tuple-element.10.norm_in), custom_call_target="tpu_custom_call" | custom-call | tf_op jit(solution)/shard_map/finish/pallas_call | solution.py:487

commit v4 on v3

--- a/solution.py
+++ b/solution.py
@@ -109,14 +109,14 @@
             pltpu.make_async_copy(
                 ref.at[:, chunk * TILE : (chunk + 1) * TILE, :],
                 fields.at[chunk, which, pl.ds(0, krylov_len)],
-                load_sem.at[chunk // 2],
+                load_sem.at[min(chunk // 2, 1)],
             ).start()
 
     def land(ref, sem):
         pltpu.make_async_copy(ref, ref, sem).wait()
 
-    def load_wait(step):
-        land(fields.at[pl.ds(2 * step, 2), :, pl.ds(0, krylov_len)], load_sem.at[step])
+    def load_wait(start, count):
+        land(fields.at[pl.ds(start, count), :, pl.ds(0, krylov_len)], load_sem.at[min(start, 1)])
 
     if padded_len > krylov_len:
         for chunk in range(chunks):
@@ -231,13 +231,13 @@
         lanes = pl.ds(pl.multiple_of(source * inner_dev, inner_dev), inner_dev)
         (ritz_ref, resid_ref)[kind][:, span, lanes] = cols
 
-    def data_copy(mask, start, count=2):
-        span = pl.ds(start, count)
+    def data_copy(mask, start, final=0):
+        span = pl.ds(start, 2)
         return pltpu.make_async_remote_copy(
             src_ref=coded.at[mask - 1, span],
             dst_ref=received.at[mask - 1, span],
             send_sem=send_sem,
-            recv_sem=recv_sem.at[mask - 1, lax.div(start, 2)],
+            recv_sem=recv_sem.at[mask - 1, final],
             device_id=device(mask, plane, core),
             device_id_type=MESH,
         )
@@ -293,9 +293,13 @@
                 stat_send[slot] = scales[part]
 
     nothing = jnp.zeros((pair, LANES), jnp.float32)
+    load_wait(0, 2)
     shift_values = prepare((1, 2))
+    stats = compute((1, 2), shift_values, 0, 2, nothing)
+    for mask in (2, 1):
+        data_copy(mask, 0).start()
+    load_wait(2, chunks - 2)
     def first(step, stats):
-        load_wait(step)
         stats = compute((1, 2), shift_values, 2 * step, 2, stats)
         @pl.when(step < pairs - 1)
         def _():
@@ -304,11 +308,15 @@
 
         return stats
 
-    stats = lax.fori_loop(0, pairs, first, nothing)
+    stats = lax.fori_loop(1, pairs, first, stats)
     finish_stats((1, 2), stats)
     for mask in (1, 2):
         stat_copy(mask).start()
-    data_copy(2, chunks - 2).start()
+
+    @pl.when(core == 0)
+    def _():
+        data_copy(2, chunks - 2, 1).start()
+
 
     coef_wait(3)
     if planes > 1:
@@ -355,8 +363,13 @@
         data_copy(3, 2 * step).start()
         return carry
 
-    lax.fori_loop(cdiv(pairs, 2), pairs, across, 0)
-    data_copy(1, chunks - 2).start()
+    lax.fori_loop(cdiv(pairs, 2), pairs - 1, across, 0)
+    data_copy(3, chunks - 2, 1).start()
+
+    @pl.when(core == 0)
+    def _():
+        data_copy(1, chunks - 2, 1).start()
+
 
     if planes > 1:
         @pl.when(plane < planes - 1)
@@ -368,9 +381,11 @@
 
     lane_dev = grid_iota((wanted_dev, LANES), 1)
 
+    def arrive(mask, final):
+        span = pl.ds(chunks - 2, 2) if final else pl.ds(0, chunks - 2)
+        land(received.at[mask - 1, span], recv_sem.at[mask - 1, final])
+
     def take(masks, step, carry):
-        for mask in masks:
-            land(received.at[mask - 1, pl.ds(2 * step, 2)], recv_sem.at[mask - 1, step])
         for half in range(2):
             chunk = 2 * step + half
             for mask in masks:
@@ -383,10 +398,20 @@
                     put_out(kind, chunk, partner(mask), size * expand_rows(scale * (1.0 / PEAK), inner_dev))
         return carry
 
+    for mask in (1, 2):
+        arrive(mask, 0)
+
+    @pl.when(lead)
+    def _():
+        data_copy(2, chunks - 2, 1).start()
+        data_copy(1, chunks - 2, 1).start()
+
     lax.fori_loop(0, pairs - 1, functools.partial(take, (1, 2)), 0)
+    land(stat_recv.at[3], small_recv.at[2])
+    arrive(3, 0)
+    lax.fori_loop(0, pairs - 1, functools.partial(take, (3,)), 0)
+    arrive(2, 1)
     take((2,), pairs - 1, 0)
-    land(stat_recv.at[3], small_recv.at[2])
-    lax.fori_loop(0, pairs, functools.partial(take, (3,)), 0)
 
     others = groups * rows - 1
     land(square_recv.at[pl.ds(0, others)], small_recv.at[1])
@@ -413,6 +438,9 @@
         for kind, ref in enumerate((coefs, values)):
             land(ref, coef_send.at[kind])
 
+    arrive(3, 1)
+    take((3,), pairs - 1, 0)
+    arrive(1, 1)
     take((1,), pairs - 1, 0)
     land(coded, send_sem)
 
@@ -472,9 +500,9 @@
             dma((2,)),
             dma((2,)),
             dma((groups - 1, 2)),
-            dma((chunks // 2,)),
+            dma((2,)),
             dma,
-            dma((groups - 1, chunks // 2)),
+            dma((groups - 1, 2)),
             dma((2,)),
             dma((3,)),
             regular,

time: 22.8 us -> 22.4 us (0.982)
  Pallas kernels: 22 us -> 21.6 us
    pallas_call x1, Pallas kernels: 20.7 us -> 20.2 us  [body(): pl.pallas_call(functools.partial(exchange_kernel, groups, rows, rows_tota...]
where the time goes in v4:
time: 22.4 us; the launch traced here: 22.2 us
  Pallas kernels  21.6 us (96%)
  between operations  0.64 us (3%)
    pallas_call x1, Pallas kernels, body(): pl.pallas_call(functools.partial(exchange_kernel, groups, rows, rows_tota...  20.2 us
    pallas_call x1, Pallas kernels, body(): pl.pallas_call(finish_kernel, name='finish', out_shape=(out, out, jax.Sha...  1.33 us

profile of v4, /device:TPU:0, one launch (start us, length us, event | category | flops | bytes accessed | tf_op | source)
XLA Modules:
  0.0 22.2 jit_solution(9133988175180443323)
XLA Ops:
  0.6 20.2 %exchange.1 = (f32[8,64,512]{2,1,0:T(8,128)S(1)}, f32[8,64,512]{2,1,0:T(8,128)S(1)}, f32[8,128]{1,0:T(8,128)S(1)}, f32[1,128]{1,0:T(1,128)S(1)}) custom-call(bf16[8,300]{1,0:T(8,128)(2,1)} %bitcast.2, bf16[1,8]{1,0:T(2,128)(2,1)} %bitcast.3, bf16[300,64,128]{2,1,0:T(8,128)(2,1)} %basis_ref.1, bf16[300,64,128]{2,1,0:T(8,128)(2,1)} %image_ref.1), custom_call_target="tpu_custom_call" | custom-call | tf_op jit(solution)/shard_map/exchange/pallas_call | solution.py:480
  20.9 1.3 %finish.1 = (f32[8,64,512]{2,1,0:T(8,128)}, f32[8,64,512]{2,1,0:T(8,128)}, f32[8]{0:T(128)}) custom-call(f32[8,64,512]{2,1,0:T(8,128)S(1)} %get-tuple-element.7.ritz_in, f32[8,64,512]{2,1,0:T(8,128)S(1)} %get-tuple-element.8.resid_in, f32[8,128]{1,0:T(8,128)S(1)} %get-tuple-element.9.factor_ref, f32[1,128]{1,0:T(1,128)S(1)} %get-tuple-element.10.norm_in), custom_call_target="tpu_custom_call" | custom-call | tf_op jit(solution)/shard_map/finish/pallas_call | solution.py:515

commit v5 on v4

--- a/solution.py
+++ b/solution.py
@@ -67,6 +67,7 @@
     core = lax.rem(row, 2)
     plane = lax.div(row, 2)
     lead = core == 1
+    last_group = jnp.where(grp == groups - 1, 1, 0)
 
     def partner(mask):
         if mask == 0:
@@ -196,7 +197,7 @@
                 expanded[:, step * wide : (step + 1) * wide] = spot.reshape(pair * TILE, wide).astype(jnp.bfloat16)
         return shift_values
 
-    def compute(slots, shift_values, start, count, stats):
+    def compute(slots, shift_values, start, count, stats, after=None):
         both = jnp.concatenate(
             [
                 fields[start + more, which].reshape(padded_len * TILE, inner_dev)
@@ -224,6 +225,8 @@
                         coded[slot - 1, chunk, :, kind * inner_dev : (kind + 1) * inner_dev] = encode(
                             cols[part], inverse[part]
                         ).reshape(block, inner_dev).astype(jnp.bfloat16)
+            if after is not None:
+                after(chunk)
         return stats
 
     def put_out(kind, chunk, source, cols):
@@ -231,8 +234,8 @@
         lanes = pl.ds(pl.multiple_of(source * inner_dev, inner_dev), inner_dev)
         (ritz_ref, resid_ref)[kind][:, span, lanes] = cols
 
-    def data_copy(mask, start, final=0):
-        span = pl.ds(start, 2)
+    def data_copy(mask, start, final=0, count=2):
+        span = pl.ds(start, count)
         return pltpu.make_async_remote_copy(
             src_ref=coded.at[mask - 1, span],
             dst_ref=received.at[mask - 1, span],
@@ -295,16 +298,22 @@
     nothing = jnp.zeros((pair, LANES), jnp.float32)
     load_wait(0, 2)
     shift_values = prepare((1, 2))
-    stats = compute((1, 2), shift_values, 0, 2, nothing)
-    for mask in (2, 1):
-        data_copy(mask, 0).start()
+
+    def send_chunk(chunk):
+        for mask in (2, 1):
+            data_copy(mask, chunk, count=1).start()
+
+    stats = compute((1, 2), shift_values, 0, 2, nothing, send_chunk)
     load_wait(2, chunks - 2)
     def first(step, stats):
         stats = compute((1, 2), shift_values, 2 * step, 2, stats)
         @pl.when(step < pairs - 1)
         def _():
-            for mask in (1, 2):
-                data_copy(mask, 2 * step).start()
+            data_copy(2, 2 * step).start()
+
+        @pl.when(step < pairs - 1 - last_group)
+        def _():
+            data_copy(1, 2 * step).start()
 
         return stats
 
@@ -340,9 +349,13 @@
     def second(step, stats):
         stats = compute((3, 0), shift_other, 2 * step, 2, stats)
 
-        @pl.when(lax.rem(step, 2) == 0)
+        @pl.when(jnp.logical_and(last_group == 0, lax.rem(step, 2) == 0))
         def _():
             data_copy(3, step).start()
+
+        @pl.when(jnp.logical_and(last_group == 1, step < pairs - 1))
+        def _():
+            data_copy(3, 2 * step).start()
 
         return stats
 
@@ -363,8 +376,13 @@
         data_copy(3, 2 * step).start()
         return carry
 
-    lax.fori_loop(cdiv(pairs, 2), pairs - 1, across, 0)
+    lax.fori_loop(jnp.where(last_group == 1, pairs - 1, cdiv(pairs, 2)), pairs - 1, across, 0)
     data_copy(3, chunks - 2, 1).start()
+
+    @pl.when(last_group == 1)
+    def _():
+        data_copy(1, chunks - 4).start()
+
 
     @pl.when(core == 0)
     def _():
@@ -376,6 +394,11 @@
         def _():
             agree(1, planes - 1 - plane)
             lax.fori_loop(plane + 1, planes, far_squares, 0)
+
+    @pl.when(lead)
+    def _():
+        data_copy(2, chunks - 2, 1).start()
+        data_copy(1, chunks - 2, 1).start()
 
     land(stat_recv.at[pl.ds(1, 2)], small_recv.at[0])
 
@@ -398,14 +421,9 @@
                     put_out(kind, chunk, partner(mask), size * expand_rows(scale * (1.0 / PEAK), inner_dev))
         return carry
 
-    for mask in (1, 2):
-        arrive(mask, 0)
-
-    @pl.when(lead)
-    def _():
-        data_copy(2, chunks - 2, 1).start()
-        data_copy(1, chunks - 2, 1).start()
-
+    arrive(2, 0)
+
+    arrive(1, 0)
     lax.fori_loop(0, pairs - 1, functools.partial(take, (1, 2)), 0)
     land(stat_recv.at[3], small_recv.at[2])
     arrive(3, 0)

time: 22.4 us -> 22.3 us (level)
  no operation moved by 1% of the time
where the time goes in v5:
time: 22.3 us; the launch traced here: 22.1 us
  Pallas kernels  21.5 us (96%)
  between operations  0.64 us (3%)
    pallas_call x1, Pallas kernels, body(): pl.pallas_call(functools.partial(exchange_kernel, groups, rows, rows_tota...  20.2 us
    pallas_call x1, Pallas kernels, body(): pl.pallas_call(finish_kernel, name='finish', out_shape=(out, out, jax.Sha...  1.33 us

profile of v5, /device:TPU:0, one launch (start us, length us, event | category | flops | bytes accessed | tf_op | source)
XLA Modules:
  0.0 22.1 jit_solution(11813848602334859433)
XLA Ops:
  0.6 20.2 %exchange.1 = (f32[8,64,512]{2,1,0:T(8,128)S(1)}, f32[8,64,512]{2,1,0:T(8,128)S(1)}, f32[8,128]{1,0:T(8,128)S(1)}, f32[1,128]{1,0:T(1,128)S(1)}) custom-call(bf16[8,300]{1,0:T(8,128)(2,1)} %bitcast.2, bf16[1,8]{1,0:T(2,128)(2,1)} %bitcast.3, bf16[300,64,128]{2,1,0:T(8,128)(2,1)} %basis_ref.1, bf16[300,64,128]{2,1,0:T(8,128)(2,1)} %image_ref.1), custom_call_target="tpu_custom_call" | custom-call | tf_op jit(solution)/shard_map/exchange/pallas_call | solution.py:498
  20.8 1.3 %finish.1 = (f32[8,64,512]{2,1,0:T(8,128)}, f32[8,64,512]{2,1,0:T(8,128)}, f32[8]{0:T(128)}) custom-call(f32[8,64,512]{2,1,0:T(8,128)S(1)} %get-tuple-element.7.ritz_in, f32[8,64,512]{2,1,0:T(8,128)S(1)} %get-tuple-element.8.resid_in, f32[8,128]{1,0:T(8,128)S(1)} %get-tuple-element.9.factor_ref, f32[1,128]{1,0:T(1,128)S(1)} %get-tuple-element.10.norm_in), custom_call_target="tpu_custom_call" | custom-call | tf_op jit(solution)/shard_map/finish/pallas_call | solution.py:533

commit v6 on v5

--- a/solution.py
+++ b/solution.py
@@ -456,10 +456,9 @@
         for kind, ref in enumerate((coefs, values)):
             land(ref, coef_send.at[kind])
 
+    arrive(1, 1)
     arrive(3, 1)
-    take((3,), pairs - 1, 0)
-    arrive(1, 1)
-    take((1,), pairs - 1, 0)
+    take((3, 1), pairs - 1, 0)
     land(coded, send_sem)
 
 

time: 22.3 us -> 22.3 us (level)
  no operation moved by 1% of the time
where the time goes in v6:
time: 22.3 us; the launch traced here: 22.1 us
  Pallas kernels  21.4 us (96%)
  between operations  0.64 us (3%)
    pallas_call x1, Pallas kernels, body(): pl.pallas_call(functools.partial(exchange_kernel, groups, rows, rows_tota...  20.1 us
    pallas_call x1, Pallas kernels, body(): pl.pallas_call(finish_kernel, name='finish', out_shape=(out, out, jax.Sha...  1.33 us

profile of v6, /device:TPU:0, one launch (start us, length us, event | category | flops | bytes accessed | tf_op | source)
XLA Modules:
  0.0 22.1 jit_solution(8526162175112543891)
XLA Ops:
  0.6 20.1 %exchange.1 = (f32[8,64,512]{2,1,0:T(8,128)S(1)}, f32[8,64,512]{2,1,0:T(8,128)S(1)}, f32[8,128]{1,0:T(8,128)S(1)}, f32[1,128]{1,0:T(1,128)S(1)}) custom-call(bf16[8,300]{1,0:T(8,128)(2,1)} %bitcast.2, bf16[1,8]{1,0:T(2,128)(2,1)} %bitcast.3, bf16[300,64,128]{2,1,0:T(8,128)(2,1)} %basis_ref.1, bf16[300,64,128]{2,1,0:T(8,128)(2,1)} %image_ref.1), custom_call_target="tpu_custom_call" | custom-call | tf_op jit(solution)/shard_map/exchange/pallas_call | solution.py:497
  20.7 1.3 %finish.1 = (f32[8,64,512]{2,1,0:T(8,128)}, f32[8,64,512]{2,1,0:T(8,128)}, f32[8]{0:T(128)}) custom-call(f32[8,64,512]{2,1,0:T(8,128)S(1)} %get-tuple-element.7.ritz_in, f32[8,64,512]{2,1,0:T(8,128)S(1)} %get-tuple-element.8.resid_in, f32[8,128]{1,0:T(8,128)S(1)} %get-tuple-element.9.factor_ref, f32[1,128]{1,0:T(1,128)S(1)} %get-tuple-element.10.norm_in), custom_call_target="tpu_custom_call" | custom-call | tf_op jit(solution)/shard_map/finish/pallas_call | solution.py:532

commit v7 on v6

--- a/solution.py
+++ b/solution.py
@@ -148,8 +148,8 @@
 
     own_sends = [
         copy
-        for mask in (1, 2)
-        for at_core in (1, 0)
+        for mask in (2, 1)
+        for at_core in (0, 1)
         for copy in coef_copies(0, mask, mask, at_core)
     ]
     relay_sends = [copy for at_core in (1, 0) for copy in coef_copies(1, 3, 2, at_core)]
@@ -319,7 +319,7 @@
 
     stats = lax.fori_loop(1, pairs, first, stats)
     finish_stats((1, 2), stats)
-    for mask in (1, 2):
+    for mask in (2, 1):
         stat_copy(mask).start()
 
     @pl.when(core == 0)

time: 22.3 us -> 22.2 us (level)
  no operation moved by 1% of the time
where the time goes in v7:
time: 22.2 us; the launch traced here: 22 us
  Pallas kernels  21.4 us (96%)
  between operations  0.64 us (3%)
    pallas_call x1, Pallas kernels, body(): pl.pallas_call(functools.partial(exchange_kernel, groups, rows, rows_tota...  20.1 us
    pallas_call x1, Pallas kernels, body(): pl.pallas_call(finish_kernel, name='finish', out_shape=(out, out, jax.Sha...  1.33 us

profile of v7, /device:TPU:0, one launch (start us, length us, event | category | flops | bytes accessed | tf_op | source)
XLA Modules:
  0.0 22.0 jit_solution(15557419650290516555)
XLA Ops:
  0.6 20.1 %exchange.1 = (f32[8,64,512]{2,1,0:T(8,128)S(1)}, f32[8,64,512]{2,1,0:T(8,128)S(1)}, f32[8,128]{1,0:T(8,128)S(1)}, f32[1,128]{1,0:T(1,128)S(1)}) custom-call(bf16[8,300]{1,0:T(8,128)(2,1)} %bitcast.2, bf16[1,8]{1,0:T(2,128)(2,1)} %bitcast.3, bf16[300,64,128]{2,1,0:T(8,128)(2,1)} %basis_ref.1, bf16[300,64,128]{2,1,0:T(8,128)(2,1)} %image_ref.1), custom_call_target="tpu_custom_call" | custom-call | tf_op jit(solution)/shard_map/exchange/pallas_call | solution.py:497
  20.7 1.3 %finish.1 = (f32[8,64,512]{2,1,0:T(8,128)}, f32[8,64,512]{2,1,0:T(8,128)}, f32[8]{0:T(128)}) custom-call(f32[8,64,512]{2,1,0:T(8,128)S(1)} %get-tuple-element.7.ritz_in, f32[8,64,512]{2,1,0:T(8,128)S(1)} %get-tuple-element.8.resid_in, f32[8,128]{1,0:T(8,128)S(1)} %get-tuple-element.9.factor_ref, f32[1,128]{1,0:T(1,128)S(1)} %get-tuple-element.10.norm_in), custom_call_target="tpu_custom_call" | custom-call | tf_op jit(solution)/shard_map/finish/pallas_call | solution.py:532
